TPU v7x, 256 devices: a 4x2x16 block of a 4x16x16 slice. The times are simulated.
256 devices in a mesh: job: 2 (over y), fsdp: 64 (over x, z), tp: 2 (over core).
Axes of the slice: x: 4, y: 2, z: 16, core: 2. Of those that a mesh axis runs over, the one named last changes fastest.
The devices are a block of a 4x16x16 slice.
Arguments:
- weight: bfloat16 [8192, 16384], P(('job', 'fsdp'), 'tp'), parts along dimension 0, may hold values from -0.09375 to 0.09375
- grad: bfloat16 [8192, 16384], P(('job', 'fsdp'), 'tp'), parts along dimension 0, may hold values from -36 to 36
- row_moment: float32 [8192], P(('job', 'fsdp')), parts along dimension 0, may hold values from 0.01 to 10
- col_moment: float32 [32768], P(('job', 'tp')), parts along dimension 0, may hold values from 0.01 to 10
- states: bfloat16 [6144, 4096], P(('job', 'fsdp')), parts along dimension 0, may hold values from -6 to 6
- norm_gain: bfloat16 [8192], P('job'), parts along dimension 0, may hold values from 0.099609375 to 1.8984375
- gate_values: bfloat16 [6144, 16384], P(('job', 'fsdp'), 'tp'), parts along dimension 0, may hold values from -8 to 8
Outputs:
- new_weight: bfloat16 [8192, 16384], P(('job', 'fsdp'), 'tp'), parts along dimension 0
- new_rows: float32 [8192], P(('job', 'fsdp')), parts along dimension 0
- new_columns: float32 [32768], P(('job', 'tp')), parts along dimension 0
- hidden: bfloat16 [6144, 16384], P(('job', 'fsdp'), 'tp'), parts along dimension 0
There are 2 independent parts, one for each index of `job`. A program takes and returns all parts, laid end to end along the dimension named above; each array names one. Nothing has to cross between parts.
All inputs are finite; a program needn't handle non-finite values.
Results may differ from a plain program's by a relative error of at most 0.002.
The roundings to bfloat16 on the way count: a program that leaves them out, or rounds other values in their place, can miss the bound.
Values may be sent and summed in bfloat16 or wider, within the bound.
No kernel may reach another device: no remote copies, remote signals or barrier semaphores. Data moves between devices by JAX's collectives and lax.ppermute only.
A program may use at most 128 MiB of HBM per device.

v0:
```python
import jax
import jax.numpy as jnp
from jax import lax
from jax.sharding import Mesh
from jax.sharding import PartitionSpec as P

JOB_FSDP = ("job", "fsdp_0", "fsdp_1")
X, Z = "fsdp_0", "fsdp_1"
CHUNKS = 2


def from_each(x, axis):
    size, me = lax.axis_size(axis), lax.axis_index(axis)
    yield me, x
    for step in sorted(range(1, size), key=lambda k: min(k, size - k)):
        moved = lax.ppermute(x, axis, [(i, (i + step) % size) for i in range(size)])
        yield lax.rem(me - step + size, size), moved


def scatter_sum(x, axis):
    size, me = lax.axis_size(axis), lax.axis_index(axis)
    blocks = x.reshape(size, -1)
    total = lax.dynamic_index_in_dim(blocks, me, 0, keepdims=False)
    for step in sorted(range(1, size), key=lambda k: min(k, size - k)):
        block = lax.dynamic_index_in_dim(blocks, lax.rem(me + step, size), 0, keepdims=False)
        total += lax.ppermute(block, axis, [(i, (i + step) % size) for i in range(size)])
    return total


def gather(x, axis):
    out = jnp.zeros((lax.axis_size(axis), *x.shape), x.dtype)
    for source, moved in from_each(x, axis):
        out = lax.dynamic_update_index_in_dim(out, moved, source, 0)
    return out


def dot(a, b):
    return jnp.dot(a, b, preferred_element_type=jnp.float32)


def step(weight, grad, row_moment, col_moment, states, norm_gain, gate_values):
    n_x, n_z, n_tp = lax.axis_size(X), lax.axis_size(Z), lax.axis_size("tp")
    local_rows, local_columns = grad.shape
    columns = local_columns * n_tp
    rows = local_rows * n_x * n_z
    gradient = grad.astype(jnp.float32)
    squares = gradient * gradient + 1e-30
    row_partial = jnp.sum(squares, axis=1)
    col_partial = jnp.sum(squares, axis=0)
    states, col_partial = lax.optimization_barrier((states, col_partial))
    values = states.astype(jnp.float32)
    scale = lax.rsqrt(jnp.mean(values * values, axis=1, keepdims=True) + 1e-06)
    share = states.shape[1] // n_tp
    my_share = lax.axis_index("tp") * share
    normed = (
        lax.dynamic_slice_in_dim(states, my_share, share, 1).astype(jnp.float32)
        * scale
        * lax.dynamic_slice_in_dim(norm_gain, my_share, share, 0).astype(jnp.float32)
    ).astype(jnp.bfloat16)
    tokens = lax.all_gather(normed, Z, axis=0, tiled=True)
    other_tokens = lax.ppermute(tokens, "tp", [(0, 1), (1, 0)])
    row_total = row_partial + lax.ppermute(row_partial, "tp", [(0, 1), (1, 0)])
    new_rows = 0.8 * row_moment + 0.2 * (row_total / columns)
    mine = jnp.concatenate([scatter_sum(col_partial, X), jnp.full((128,), jnp.sum(new_rows) / 128)])
    mine = lax.all_to_all(jnp.broadcast_to(mine, (n_z, *mine.shape)), Z, 0, 0).sum(axis=0)
    quarters = gather(mine, X)
    col_total = quarters[:, :-128].reshape(-1)
    rows_summed = jnp.sum(quarters[:, -128:])
    new_columns = 0.8 * col_moment + 0.2 * (col_total / rows)
    row_scale = rows_summed / rows
    update = gradient / jnp.sqrt(new_rows[:, None] * new_columns[None, :] / row_scale)
    new_weight = (weight.astype(jnp.float32) - 0.01 * update).astype(jnp.bfloat16)

    width = local_columns // CHUNKS
    hidden, ups = [], []
    for c in range(CHUNKS):
        part = slice(c * width, (c + 1) * width)
        block = lax.all_to_all(new_weight[:, part], Z, split_axis=1, concat_axis=0, tiled=True)
        if ups:
            block, ups[-1] = lax.optimization_barrier((block, ups[-1]))
        block = gather(block, X).reshape(rows, -1)
        up = dot(tokens, lax.dynamic_slice_in_dim(block, my_share, share, 0))
        up += dot(other_tokens, lax.dynamic_slice_in_dim(block, share - my_share, share, 0))
        ups.append(up.astype(jnp.bfloat16))
    for c, up in enumerate(ups):
        part = slice(c * width, (c + 1) * width)
        up = lax.all_to_all(up, Z, split_axis=0, concat_axis=1, tiled=True)
        gate = jax.nn.silu(gate_values[:, part].astype(jnp.float32))
        hidden.append((gate * up.astype(jnp.float32)).astype(jnp.bfloat16))
    return (new_weight, new_rows, new_columns, jnp.concatenate(hidden, axis=1))


def solution(mesh):
    job, fsdp, tp = (mesh.shape[n] for n in ("job", "fsdp", "tp"))
    finer = Mesh(mesh.devices.reshape(job, 4, fsdp // 4, tp), ("job", X, Z, "tp"))
    placed = (
        P(JOB_FSDP, "tp"),
        P(JOB_FSDP, "tp"),
        P(JOB_FSDP),
        P(("job", "tp")),
        P(JOB_FSDP, None),
        P("job"),
        P(JOB_FSDP, "tp"),
    )
    return jax.shard_map(
        step,
        mesh=finer,
        in_specs=placed,
        out_specs=(P(JOB_FSDP, "tp"), P(JOB_FSDP), P(("job", "tp")), P(JOB_FSDP, "tp")),
        check_vma=False,
    )
```

profile of v0, /device:TPU:46, one launch (start us, length us, event | category | flops | bytes accessed | tf_op | source)
XLA Modules:
  0.0 235.5 jit_solution(8416749424340409858)
XLA Ops:
  7.2 0.1 all-gather.2.cloned.1.call-start
  7.3 1.9 fusion.2
  9.2 1.2 multiply_reduce_fusion
  10.3 0.7 dynamic-slice_convert_fusion
  11.0 1.7 multiply_convert_fusion
  12.8 0.1 all-gather.2.cloned.1.call-update
  12.9 0.2 collective-permute-start.1
  13.1 0.1 collective-permute-start
  13.2 1.9 collective-permute-start.2
  15.1 1.1 collective-permute-start.3
  16.2 0.0 collective-permute-done
  16.2 0.6 fusion.29
  17.5 0.0 collective-permute-done.1
  17.5 0.7 collective-permute-done.2
  18.2 2.0 collective-permute-done.3
  20.2 0.1 broadcast_in_dim.50
  20.3 39.2 %all_to_all.70 = f32[16,1,2176]{2,1,0:T(1,128)S(1)} all-to-all(f32[16,1,2176]{2,1,0:T(1,128)S(1)} %broadcast_in_dim.50), channel_id=1, replica_groups=mesh['job'=2,'fsdp_0'=4,'fsdp_1'=16,'tp'=2] {'fsdp_1'}, dimensions={0} | all-to-all | bytes 278528 | tf_op jit(solution)/shard_map/all_to_all | solution.py:65
  59.5 0.1 reduce_sum.57
  59.6 1.8 collective-permute-start.4
  61.4 0.3 collective-permute-start.5
  61.7 1.3 collective-permute-start.6
  63.0 0.1 dynamic_update_slice.38
  63.2 0.2 collective-permute-done.4
  63.4 0.1 dynamic_update_slice.39
  63.5 2.8 %collective-permute-done.5 = f32[2176]{0:T(1024)S(1)} collective-permute-done((f32[2176]{0:T(1024)S(1)}, f32[2176]{0:T(1024)S(1)}, u32[]{:S(2)}, u32[]{:S(2)}) %collective-permute-start.5) | collective-permute-done | bytes 8736 | tf_op jit(solution)/shard_map/ppermute | solution.py:16
  66.3 0.1 dynamic_update_slice.40
  66.5 0.5 collective-permute-done.6
  66.9 0.1 dynamic_update_slice.41
  67.1 0.6 slice_reduce_fusion
  68.4 0.0 copy-start.4
  68.4 0.7 fusion.5
  69.1 0.0 copy-start.1
  69.1 0.1 fusion.30
  69.2 1.0 copy.41
  70.2 4.8 %all-to-all-start.2 = ((bf16[64,16,256]{2,0,1:T(8,128)(2,1)}), bf16[64,16,256]{2,0,1:T(8,128)(2,1)S(1)}, u32[]{:S(2)}, u32[]{:S(2)}) async-start(bf16[64,16,256]{2,0,1:T(8,128)(2,1)} %bitcast.51), calls=%async_computation.2 | async-start | bytes 1048576 | tf_op jit(solution)/shard_map/all_to_all | solution.py:78
  75.1 46.9 %all-gather.2.cloned.1.call-done = bf16[768,2048]{1,0:T(8,128)(2,1)} async-done(((bf16[48,2048]{1,0:T(8,128)(2,1)}), bf16[768,2048]{1,0:T(8,128)(2,1)}) %all-gather.2.cloned.1.call-update) | async-done | bytes 3145744 | tf_op jit(solution)/shard_map/all_gather | solution.py:60
  122.0 0.6 collective-permute-start.7
  122.5 0.8 copy.42
  123.4 7.8 %all-to-all-start.1 = ((bf16[64,16,256]{2,0,1:T(8,128)(2,1)}), bf16[64,16,256]{2,0,1:T(8,128)(2,1)S(1)}, u32[]{:S(2)}, u32[]{:S(2)}) async-start(bf16[64,16,256]{2,0,1:T(8,128)(2,1)} %bitcast.52), calls=%async_computation.1 | async-start | bytes 1048576 | tf_op jit(solution)/shard_map/all_to_all | solution.py:78
  131.2 0.6 collective-permute-start.8
  131.8 1.6 collective-permute-start.9
  133.4 0.1 broadcast.37.clone
  133.6 3.1 %collective-permute-done.7 = bf16[1024,256]{1,0:T(8,128)(2,1)S(1)} collective-permute-done((bf16[1024,256]{1,0:T(8,128)(2,1)S(1)}, bf16[1024,256]{1,0:T(8,128)(2,1)S(1)}, u32[]{:S(2)}, u32[]{:S(2)}) %collective-permute-start.7) | collective-permute-done | bytes 524320 | tf_op jit(solution)/shard_map/ppermute | solution.py:16
  136.8 20.7 %collective-permute-done.8 = bf16[1024,256]{1,0:T(8,128)(2,1)S(1)} collective-permute-done((bf16[1024,256]{1,0:T(8,128)(2,1)S(1)}, bf16[1024,256]{1,0:T(8,128)(2,1)S(1)}, u32[]{:S(2)}, u32[]{:S(2)}) %collective-permute-start.8) | collective-permute-done | bytes 524320 | tf_op jit(solution)/shard_map/ppermute | solution.py:16
  157.7 3.0 %fusion.11 = f32[768,256]{1,0:T(8,128)S(1)} fusion(bf16[768,2048]{1,0:T(8,128)(2,1)} %collective-permute-done.10, bf16[4096,256]{1,0:T(8,128)(2,1)S(1)} %bitcast.57, s32[]{:T(128)S(6)} %select_n.42), kind=kOutput, calls=%fused_computation.15 | convolution fusion | flops 805306368 | bytes 4980740 | tf_op jit(solution)/shard_map/dot_general | solution.py:38
  160.7 1.7 fusion.6
  162.5 2.0 collective-permute-start.12
  164.5 0.7 collective-permute-start.13
  165.2 11.6 %all-to-all-start.3 = ((bf16[16,48,256]{2,1,0:T(8,128)(2,1)}), bf16[16,48,256]{2,1,0:T(8,128)(2,1)S(1)}, u32[]{:S(2)}, u32[]{:S(2)}) async-start(bf16[16,48,256]{2,1,0:T(8,128)(2,1)} %bitcast.14), calls=%async_computation.3 | async-start | bytes 786432 | tf_op jit(solution)/shard_map/all_to_all | solution.py:87
  176.9 0.1 broadcast.37
  177.1 0.2 collective-permute-done.11
  177.4 9.7 %collective-permute-done.13 = bf16[1024,256]{1,0:T(8,128)(2,1)S(1)} collective-permute-done((bf16[1024,256]{1,0:T(8,128)(2,1)S(1)}, bf16[1024,256]{1,0:T(8,128)(2,1)S(1)}, u32[]{:S(2)}, u32[]{:S(2)}) %collective-permute-start.13) | collective-permute-done | bytes 524320 | tf_op jit(solution)/shard_map/ppermute | solution.py:16
  187.1 3.0 %fusion.8 = f32[768,256]{1,0:T(8,128)S(1)} fusion(bf16[768,2048]{1,0:T(8,128)(2,1)} %collective-permute-done.10, bf16[4096,256]{1,0:T(8,128)(2,1)S(1)} %bitcast.55, s32[]{:T(128)S(6)} %select_n.42), kind=kOutput, calls=%fused_computation.12 | convolution fusion | flops 805306368 | bytes 4980740 | tf_op jit(solution)/shard_map/dot_general | solution.py:38
  190.2 1.7 fusion.7
  191.9 6.2 %all-to-all-done.3 = bf16[16,48,256]{2,1,0:T(8,128)(2,1)S(1)} async-done(((bf16[16,48,256]{2,1,0:T(8,128)(2,1)}), bf16[16,48,256]{2,1,0:T(8,128)(2,1)S(1)}, u32[]{:S(2)}, u32[]{:S(2)}) %all-to-all-start.3) | async-done | bytes 393248 | tf_op jit(solution)/shard_map/all_to_all | solution.py:87
  198.1 6.7 %all-to-all-start.4 = ((bf16[16,48,256]{2,1,0:T(8,128)(2,1)}), bf16[16,48,256]{2,1,0:T(8,128)(2,1)S(1)}, u32[]{:S(2)}, u32[]{:S(2)}) async-start(bf16[16,48,256]{2,1,0:T(8,128)(2,1)} %bitcast.21), calls=%async_computation.4 | async-start | bytes 786432 | tf_op jit(solution)/shard_map/all_to_all | solution.py:87
  204.8 0.1 convert_bitcast_fusion.1
  204.9 0.0 copy-start.3
  204.9 0.1 copy.36
  205.0 22.1 %all-to-all-done.4 = bf16[16,48,256]{2,1,0:T(8,128)(2,1)S(1)} async-done(((bf16[16,48,256]{2,1,0:T(8,128)(2,1)}), bf16[16,48,256]{2,1,0:T(8,128)(2,1)S(1)}, u32[]{:S(2)}, u32[]{:S(2)}) %all-to-all-start.4) | async-done | bytes 393248 | tf_op jit(solution)/shard_map/all_to_all | solution.py:87
  227.1 0.1 convert_bitcast_fusion
  227.2 0.1 copy.37
  227.3 0.4 fusion.23
  227.7 0.9 pad_maximum_fusion
  (45 shorter events, 0.5 us)
Async XLA Ops:
  7.2 61.2 %copy-start = (bf16[64,8192]{1,0:T(8,128)(2,1)S(1)}, bf16[64,8192]{1,0:T(8,128)(2,1)}, u32[]{:S(2)}) copy-start(bf16[64,8192]{1,0:T(8,128)(2,1)} %param.8) | copy-start | bytes 3145732
  7.2 9.0 %copy-start.7 = (f32[64]{0:T(128)S(1)}, f32[64]{0:T(128)}, u32[]{:S(2)}) copy-start(f32[64]{0:T(128)} %param.9) | copy-start | bytes 772
  7.2 61.1 %copy-start.5 = (f32[8192]{0:T(1024)S(1)}, f32[8192]{0:T(1024)}, u32[]{:S(2)}) copy-start(f32[8192]{0:T(1024)} %param.10) | copy-start | bytes 98308
  7.2 61.2 %copy-start.2 = (bf16[64,8192]{1,0:T(8,128)(2,1)S(1)}, bf16[64,8192]{1,0:T(8,128)(2,1)}, u32[]{:S(2)}) copy-start(bf16[64,8192]{1,0:T(8,128)(2,1)} %param.7) | copy-start | bytes 3145732
  7.2 114.7 %all-gather.2.cloned.1.call-start = ((), (), s32[]{:S(2)}) async-start(), calls=%async_computation.5 | async-start | bytes 3342336 | tf_op jit(solution)/shard_map/all_gather | solution.py:60
  12.9 4.5 %collective-permute-start.1 = (f32[2048]{0:T(1024)S(1)}, f32[2048]{0:T(1024)S(1)}, u32[]{:S(2)}, u32[]{:S(2)}) collective-permute-start(f32[2048]{0:T(1024)S(1)} %bitcast.73), channel_id=1, source_target_pairs={{0,32},{32,64},{64,96},{96,0},{1,33},{33,65},{65,97},{97,1},{2,34}... | collective-permute-start | bytes 24584 | tf_op jit(solution)/shard_map/ppermute | solution.py:26
  13.1 3.1 %collective-permute-start = (f32[64]{0:T(128)S(1)}, f32[64]{0:T(128)S(1)}, u32[]{:S(2)}, u32[]{:S(2)}) collective-permute-start(f32[64]{0:T(128)S(1)} %get-tuple-element.12), channel_id=1, source_target_pairs={{0,1},{1,0},{2,3},{3,2},{4,5},{5,4},{6,7},{7,6},{8,9},{9,8},{10,11... | collective-permute-start | bytes 776 | tf_op jit(solution)/shard_map/ppermute | solution.py:62
  13.2 5.0 %collective-permute-start.2 = (f32[2048]{0:T(1024)S(1)}, f32[2048]{0:T(1024)S(1)}, u32[]{:S(2)}, u32[]{:S(2)}) collective-permute-start(f32[2048]{0:T(1024)S(1)} %bitcast.72), channel_id=1, source_target_pairs={{0,96},{32,0},{64,32},{96,64},{1,97},{33,1},{65,33},{97,65},{2,98}... | collective-permute-start | bytes 24584 | tf_op jit(solution)/shard_map/ppermute | solution.py:26
  15.1 5.2 %collective-permute-start.3 = (f32[2048]{0:T(1024)S(1)}, f32[2048]{0:T(1024)S(1)}, u32[]{:S(2)}, u32[]{:S(2)}) collective-permute-start(f32[2048]{0:T(1024)S(1)} %bitcast.71), channel_id=1, source_target_pairs={{0,64},{32,96},{64,0},{96,32},{1,65},{33,97},{65,1},{97,33},{2,66}... | collective-permute-start | bytes 24584 | tf_op jit(solution)/shard_map/ppermute | solution.py:26
  16.8 52.2 %copy-start.6 = (f32[64]{0:T(128)}, f32[64]{0:T(128)S(1)}, u32[]{:S(2)}) copy-start(f32[64]{0:T(128)S(1)} %get-tuple-element.15) | copy-start | bytes 772
  59.6 3.8 %collective-permute-start.4 = (f32[2176]{0:T(1024)S(1)}, f32[2176]{0:T(1024)S(1)}, u32[]{:S(2)}, u32[]{:S(2)}) collective-permute-start(f32[2176]{0:T(1024)S(1)} %reduce_sum.57), channel_id=1, source_target_pairs={{0,32},{32,64},{64,96},{96,0},{1,33},{33,65},{65,97},{97,1},{2,34}... | collective-permute-start | bytes 26120 | tf_op jit(solution)/shard_map/ppermute | solution.py:16
  61.4 4.9 %collective-permute-start.5 = (f32[2176]{0:T(1024)S(1)}, f32[2176]{0:T(1024)S(1)}, u32[]{:S(2)}, u32[]{:S(2)}) collective-permute-start(f32[2176]{0:T(1024)S(1)} %reduce_sum.57), channel_id=1, source_target_pairs={{0,96},{32,0},{64,32},{96,64},{1,97},{33,1},{65,33},{97,65},{2,98}... | collective-permute-start | bytes 26120 | tf_op jit(solution)/shard_map/ppermute | solution.py:16
  61.7 5.2 %collective-permute-start.6 = (f32[2176]{0:T(1024)S(1)}, f32[2176]{0:T(1024)S(1)}, u32[]{:S(2)}, u32[]{:S(2)}) collective-permute-start(f32[2176]{0:T(1024)S(1)} %reduce_sum.57), channel_id=1, source_target_pairs={{0,64},{32,96},{64,0},{96,32},{1,65},{33,97},{65,1},{97,33},{2,66}... | collective-permute-start | bytes 26120 | tf_op jit(solution)/shard_map/ppermute | solution.py:16
  68.4 0.8 copy-start.4
  69.1 1.2 copy-start.1
  70.2 51.7 %all-to-all-start.2 = ((bf16[64,16,256]{2,0,1:T(8,128)(2,1)}), bf16[64,16,256]{2,0,1:T(8,128)(2,1)S(1)}, u32[]{:S(2)}, u32[]{:S(2)}) async-start(bf16[64,16,256]{2,0,1:T(8,128)(2,1)} %bitcast.51), calls=%async_computation.2 | async-start | bytes 1048576 | tf_op jit(solution)/shard_map/all_to_all | solution.py:78
  122.0 35.7 %collective-permute-start.10 = (bf16[768,2048]{1,0:T(8,128)(2,1)}, bf16[768,2048]{1,0:T(8,128)(2,1)}, u32[]{:S(2)}, u32[]{:S(2)}) collective-permute-start(bf16[768,2048]{1,0:T(8,128)(2,1)} %all-gather.2.cloned.1.call-done), channel_id=1, source_target_pairs={{0,1},{1,0},{2,3},{3,2},{4,5},{5,4},{6,7},{7,6},{8,9},{9,8},{10,11... | collective-permute-start | bytes 9437192 | tf_op jit(solution)/shard_map/ppermute | solution.py:61
  122.0 14.8 %collective-permute-start.7 = (bf16[1024,256]{1,0:T(8,128)(2,1)S(1)}, bf16[1024,256]{1,0:T(8,128)(2,1)S(1)}, u32[]{:S(2)}, u32[]{:S(2)}) collective-permute-start(bf16[1024,256]{1,0:T(8,128)(2,1)S(1)} %bitcast.63), channel_id=1, source_target_pairs={{0,32},{32,64},{64,96},{96,0},{1,33},{33,65},{65,97},{97,1},{2,34}... | collective-permute-start | bytes 1572872 | tf_op jit(solution)/shard_map/ppermute | solution.py:16
  123.4 39.1 %all-to-all-start.1 = ((bf16[64,16,256]{2,0,1:T(8,128)(2,1)}), bf16[64,16,256]{2,0,1:T(8,128)(2,1)S(1)}, u32[]{:S(2)}, u32[]{:S(2)}) async-start(bf16[64,16,256]{2,0,1:T(8,128)(2,1)} %bitcast.52), calls=%async_computation.1 | async-start | bytes 1048576 | tf_op jit(solution)/shard_map/all_to_all | solution.py:78
  131.2 26.3 %collective-permute-start.8 = (bf16[1024,256]{1,0:T(8,128)(2,1)S(1)}, bf16[1024,256]{1,0:T(8,128)(2,1)S(1)}, u32[]{:S(2)}, u32[]{:S(2)}) collective-permute-start(bf16[1024,256]{1,0:T(8,128)(2,1)S(1)} %bitcast.64), channel_id=1, source_target_pairs={{0,96},{32,0},{64,32},{96,64},{1,97},{33,1},{65,33},{97,65},{2,98}... | collective-permute-start | bytes 1572872 | tf_op jit(solution)/shard_map/ppermute | solution.py:16
  131.8 25.8 %collective-permute-start.9 = (bf16[1024,256]{1,0:T(8,128)(2,1)S(1)}, bf16[1024,256]{1,0:T(8,128)(2,1)S(1)}, u32[]{:S(2)}, u32[]{:S(2)}) collective-permute-start(bf16[1024,256]{1,0:T(8,128)(2,1)S(1)} %bitcast.65), channel_id=1, source_target_pairs={{0,64},{32,96},{64,0},{96,32},{1,65},{33,97},{65,1},{97,33},{2,66}... | collective-permute-start | bytes 1572872 | tf_op jit(solution)/shard_map/ppermute | solution.py:16
  157.6 3.1 %copy-start.8 = (bf16[768,2048]{1,0:T(8,128)(2,1)S(1)}, bf16[768,2048]{1,0:T(8,128)(2,1)}, u32[]{:S(2)}) copy-start(bf16[768,2048]{1,0:T(8,128)(2,1)} %all-gather.2.cloned.1.call-done) | copy-start | bytes 9437188
  162.5 14.8 %collective-permute-start.11 = (bf16[1024,256]{1,0:T(8,128)(2,1)S(1)}, bf16[1024,256]{1,0:T(8,128)(2,1)S(1)}, u32[]{:S(2)}, u32[]{:S(2)}) collective-permute-start(bf16[1024,256]{1,0:T(8,128)(2,1)S(1)} %bitcast.59), channel_id=1, source_target_pairs={{0,32},{32,64},{64,96},{96,0},{1,33},{33,65},{65,97},{97,1},{2,34}... | collective-permute-start | bytes 1572872 | tf_op jit(solution)/shard_map/ppermute | solution.py:16
  162.5 14.8 %collective-permute-start.12 = (bf16[1024,256]{1,0:T(8,128)(2,1)S(1)}, bf16[1024,256]{1,0:T(8,128)(2,1)S(1)}, u32[]{:S(2)}, u32[]{:S(2)}) collective-permute-start(bf16[1024,256]{1,0:T(8,128)(2,1)S(1)} %bitcast.60), channel_id=1, source_target_pairs={{0,96},{32,0},{64,32},{96,64},{1,97},{33,1},{65,33},{97,65},{2,98}... | collective-permute-start | bytes 1572872 | tf_op jit(solution)/shard_map/ppermute | solution.py:16
  164.5 22.6 %collective-permute-start.13 = (bf16[1024,256]{1,0:T(8,128)(2,1)S(1)}, bf16[1024,256]{1,0:T(8,128)(2,1)S(1)}, u32[]{:S(2)}, u32[]{:S(2)}) collective-permute-start(bf16[1024,256]{1,0:T(8,128)(2,1)S(1)} %bitcast.61), channel_id=1, source_target_pairs={{0,64},{32,96},{64,0},{96,32},{1,65},{33,97},{65,1},{97,33},{2,66}... | collective-permute-start | bytes 1572872 | tf_op jit(solution)/shard_map/ppermute | solution.py:16
  165.2 32.9 %all-to-all-start.3 = ((bf16[16,48,256]{2,1,0:T(8,128)(2,1)}), bf16[16,48,256]{2,1,0:T(8,128)(2,1)S(1)}, u32[]{:S(2)}, u32[]{:S(2)}) async-start(bf16[16,48,256]{2,1,0:T(8,128)(2,1)} %bitcast.14), calls=%async_computation.3 | async-start | bytes 786432 | tf_op jit(solution)/shard_map/all_to_all | solution.py:87
  187.1 3.1 %copy-start.9 = (bf16[768,2048]{1,0:T(8,128)(2,1)S(1)}, bf16[768,2048]{1,0:T(8,128)(2,1)}, u32[]{:S(2)}) copy-start(bf16[768,2048]{1,0:T(8,128)(2,1)} %all-gather.2.cloned.1.call-done) | copy-start | bytes 9437188
  198.1 29.0 %all-to-all-start.4 = ((bf16[16,48,256]{2,1,0:T(8,128)(2,1)}), bf16[16,48,256]{2,1,0:T(8,128)(2,1)S(1)}, u32[]{:S(2)}, u32[]{:S(2)}) async-start(bf16[16,48,256]{2,1,0:T(8,128)(2,1)} %bitcast.21), calls=%async_computation.4 | async-start | bytes 786432 | tf_op jit(solution)/shard_map/all_to_all | solution.py:87
  204.9 22.4 %copy-start.3 = (bf16[48,8192]{1,0:T(8,128)(2,1)S(1)}, bf16[48,8192]{1,0:T(8,128)(2,1)}, u32[]{:S(2)}) copy-start(bf16[48,8192]{1,0:T(8,128)(2,1)} %param.13) | copy-start | bytes 2359300
Sparse Core Ops, SparseCore 0:
  12.9 108.9 all-gather.1
where the time goes:
time: 238 us; the launch traced here: 235 us
  waiting for transfers between devices  115 us (48%)
  starting transfers between devices  43.3 us (18%)
  blocking collectives  39.2 us (16%)
  between operations  15.8 us (7%)
  matrix products  9.56 us (4%)
  other arithmetic  8.95 us (4%)
  local copies, waits for them, and re-layouts  3.42 us (1%)
    all_gather x1, waiting for transfers between devices, step(): tokens = lax.all_gather(normed, Z, axis=0, tiled=True)  46.9 us
    all_to_all x1, blocking collectives, step(): lax.all_to_all(jnp.broadcast_to(mine, (n_z, *mine.shape)), Z, 0, 0)  39.2 us
    ppermute x9, waiting for transfers between devices, from_each(): moved = lax.ppermute(x, axis, [(i, (i + step) % size) for i in range(size)])  37.2 us
    all_to_all x2, waiting for transfers between devices, step(): up = lax.all_to_all(up, Z, split_axis=0, concat_axis=1, tiled=True)  28.3 us
    all_to_all x2, starting transfers between devices, step(): up = lax.all_to_all(up, Z, split_axis=0, concat_axis=1, tiled=True)  18.3 us
    all_to_all x2, starting transfers between devices, step(): lax.all_to_all(new_weight[:, part], Z, split_axis=1, concat_axis=0, tiled...  12.6 us
    dot_general x4, matrix products, dot(): return jnp.dot(a, b, preferred_element_type=jnp.float32)  9.56 us
    ppermute x9, starting transfers between devices, from_each(): moved = lax.ppermute(x, axis, [(i, (i + step) % size) for i in range(size)])  8.99 us
  transfers between devices with their start and end apart: 19, of which 12 were waited for; matrix products, arithmetic and copies ran while one was open for 6% of the time, Pallas kernels for 0%

commit v1 on v0

--- a/solution.py
+++ b/solution.py
@@ -34,6 +34,22 @@
     return out
 
 
+def ring_gather(x, axis):
+    size, me = lax.axis_size(axis), lax.axis_index(axis)
+    x = lax.optimization_barrier(x)
+    out = jnp.zeros((size, *x.shape), x.dtype)
+    out = lax.dynamic_update_index_in_dim(out, x, me, 0)
+    right = left = x
+    for step in range(1, size // 2 + 1):
+        right = lax.ppermute(right, axis, [(i, (i + 1) % size) for i in range(size)])
+        if step < size - step:
+            left = lax.ppermute(left, axis, [((i + 1) % size, i) for i in range(size)])
+        out = lax.dynamic_update_index_in_dim(out, right, lax.rem(me - step + size, size), 0)
+        if step < size - step:
+            out = lax.dynamic_update_index_in_dim(out, left, lax.rem(me + step, size), 0)
+    return out
+
+
 def dot(a, b):
     return jnp.dot(a, b, preferred_element_type=jnp.float32)
 
@@ -43,34 +59,40 @@
     local_rows, local_columns = grad.shape
     columns = local_columns * n_tp
     rows = local_rows * n_x * n_z
+    share = states.shape[1] // n_tp
+    my_share = lax.axis_index("tp") * share
+    tokens = ring_gather(lax.dynamic_slice_in_dim(states, my_share, share, 1), Z)
+    other_tokens = lax.ppermute(tokens, "tp", [(0, 1), (1, 0)])
     gradient = grad.astype(jnp.float32)
     squares = gradient * gradient + 1e-30
     row_partial = jnp.sum(squares, axis=1)
     col_partial = jnp.sum(squares, axis=0)
-    states, col_partial = lax.optimization_barrier((states, col_partial))
     values = states.astype(jnp.float32)
-    scale = lax.rsqrt(jnp.mean(values * values, axis=1, keepdims=True) + 1e-06)
-    share = states.shape[1] // n_tp
-    my_share = lax.axis_index("tp") * share
-    normed = (
-        lax.dynamic_slice_in_dim(states, my_share, share, 1).astype(jnp.float32)
-        * scale
-        * lax.dynamic_slice_in_dim(norm_gain, my_share, share, 0).astype(jnp.float32)
-    ).astype(jnp.bfloat16)
-    tokens = lax.all_gather(normed, Z, axis=0, tiled=True)
-    other_tokens = lax.ppermute(tokens, "tp", [(0, 1), (1, 0)])
+    scale = lax.rsqrt(jnp.mean(values * values, axis=1) + 1e-06)
     row_total = row_partial + lax.ppermute(row_partial, "tp", [(0, 1), (1, 0)])
     new_rows = 0.8 * row_moment + 0.2 * (row_total / columns)
-    mine = jnp.concatenate([scatter_sum(col_partial, X), jnp.full((128,), jnp.sum(new_rows) / 128)])
-    mine = lax.all_to_all(jnp.broadcast_to(mine, (n_z, *mine.shape)), Z, 0, 0).sum(axis=0)
+    quarter = scatter_sum(col_partial, X)
+    n_quarter = quarter.shape[0]
+    extra = jnp.zeros((128,), jnp.float32).at[: scale.shape[0]].set(scale)
+    extra = extra.at[-1].set(jnp.sum(new_rows))
+    mine = jnp.concatenate([quarter, extra])
+    theirs = lax.all_to_all(jnp.broadcast_to(mine, (n_z, *mine.shape)), Z, 0, 0)
+    scales = theirs[:, n_quarter : n_quarter + scale.shape[0]].reshape(-1, 1)
+    mine = theirs.sum(axis=0)
     quarters = gather(mine, X)
     col_total = quarters[:, :-128].reshape(-1)
-    rows_summed = jnp.sum(quarters[:, -128:])
+    rows_summed = jnp.sum(quarters[:, -1])
     new_columns = 0.8 * col_moment + 0.2 * (col_total / rows)
     row_scale = rows_summed / rows
     update = gradient / jnp.sqrt(new_rows[:, None] * new_columns[None, :] / row_scale)
     new_weight = (weight.astype(jnp.float32) - 0.01 * update).astype(jnp.bfloat16)
 
+    def normed(part, start):
+        gain = lax.dynamic_slice_in_dim(norm_gain, start, share, 0).astype(jnp.float32)
+        return (part.reshape(-1, share).astype(jnp.float32) * scales * gain).astype(jnp.bfloat16)
+
+    tokens = normed(tokens, my_share)
+    other_tokens = normed(other_tokens, share - my_share)
     width = local_columns // CHUNKS
     hidden, ups = [], []
     for c in range(CHUNKS):

time: 238 us -> 249 us (1.046)
  starting transfers between devices: 43.3 us -> 94.7 us
  blocking collectives: 39.2 us -> 0 us
  local copies, waits for them, and re-layouts: 3.42 us -> 22 us
  between operations: 15.8 us -> 1.96 us
  waiting for transfers between devices: 115 us -> 109 us
  matrix products: 9.56 us -> 5.45 us
  other arithmetic: 8.95 us -> 13 us
    ppermute x0 -> x15, waiting for transfers between devices: none -> 48.6 us  [the longest x8 48.6 us: ring_gather(): lax.ppermute(right, axis, [(i, (i + 1) % size) for i in range(size)])]
    all_gather x1 -> x0, waiting for transfers between devices: 46.9 us -> none  [step(): tokens = lax.all_gather(normed, Z, axis=0, tiled=True)]
    ppermute x0 -> x15, starting transfers between devices: none -> 42.4 us  [the longest x7 36.2 us: ring_gather(): left = lax.ppermute(left, axis, [((i + 1) % size, i) for i in range(size)])]
    all_to_all x1 -> x0, blocking collectives: 39.2 us -> none  [step(): lax.all_to_all(jnp.broadcast_to(mine, (n_z, *mine.shape)), Z, 0, 0)]
    ppermute x9, waiting for transfers between devices: 37.2 us -> 22.8 us  [from_each(): moved = lax.ppermute(x, axis, [(i, (i + step) % size) for i in range(size)])]
    all_to_all x2, starting transfers between devices: 12.6 us -> 19.2 us  [step(): lax.all_to_all(new_weight[:, part], Z, split_axis=1, concat_axis=0, tiled...]
    all_to_all x2, waiting for transfers between devices: 0.01 us -> 5.19 us  [step(): lax.all_to_all(new_weight[:, part], Z, split_axis=1, concat_axis=0, tiled...]
    dynamic_update_slice x0 -> x16, local copies, waits for them, and re-layouts: none -> 4.92 us  [the longest x8 2.91 us: ring_gather(): lax.dynamic_update_index_in_dim(out, right, lax.rem(me - step + size, siz...]
  transfers between devices with their start and end apart: 19 -> 34, of which waited for: 12 -> 15; matrix products, arithmetic and copies ran while one was open for 6% -> 14% of each run, Pallas kernels for 0% -> 0%
where the time goes in v1:
time: 249 us; the launch traced here: 246 us
  waiting for transfers between devices  109 us (44%)
  starting transfers between devices  94.7 us (38%)
  local copies, waits for them, and re-layouts  22 us (9%)
  other arithmetic  13 us (5%)
  matrix products  5.45 us (2%)
    ppermute x8, waiting for transfers between devices, ring_gather(): lax.ppermute(right, axis, [(i, (i + 1) % size) for i in range(size)])  48.6 us
    ppermute x7, starting transfers between devices, ring_gather(): left = lax.ppermute(left, axis, [((i + 1) % size, i) for i in range(size)])  36.2 us
    all_to_all x2, waiting for transfers between devices, step(): up = lax.all_to_all(up, Z, split_axis=0, concat_axis=1, tiled=True)  30.1 us
    ppermute x9, waiting for transfers between devices, from_each(): moved = lax.ppermute(x, axis, [(i, (i + step) % size) for i in range(size)])  22.8 us
    all_to_all x2, starting transfers between devices, step(): lax.all_to_all(new_weight[:, part], Z, split_axis=1, concat_axis=0, tiled...  19.2 us
    all_to_all x2, starting transfers between devices, step(): up = lax.all_to_all(up, Z, split_axis=0, concat_axis=1, tiled=True)  13.4 us
    ppermute x9, starting transfers between devices, from_each(): moved = lax.ppermute(x, axis, [(i, (i + step) % size) for i in range(size)])  12.1 us
    ppermute x8, starting transfers between devices, ring_gather(): lax.ppermute(right, axis, [(i, (i + 1) % size) for i in range(size)])  6.21 us
  transfers between devices with their start and end apart: 34, of which 15 were waited for; matrix products, arithmetic and copies ran while one was open for 14% of the time, Pallas kernels for 0%

profile of v1, /device:TPU:46, one launch (start us, length us, event | category | flops | bytes accessed | tf_op | source)
XLA Modules:
  0.0 246.0 jit_solution(5302045714188423777)
XLA Ops:
  0.6 0.9 constant_dynamic-slice_fusion
  1.6 2.9 %collective-permute-start.7 = (bf16[48,2048]{1,0:T(8,128)(2,1)S(1)}, bf16[48,2048]{1,0:T(8,128)(2,1)}, u32[]{:S(2)}, u32[]{:S(2)}) collective-permute-start(bf16[48,2048]{1,0:T(8,128)(2,1)S(1)} %constant_dynamic-slice_fusion), channel_id=1, source_target_pairs={{0,2},{2,4},{4,6},{6,8},{8,10},{10,12},{12,14},{14,16},{16,18},{18... | collective-permute-start | bytes 589832 | tf_op jit(solution)/shard_map/ppermute | solution.py:44
  4.5 19.7 %collective-permute-start.8 = (bf16[48,2048]{1,0:T(8,128)(2,1)S(1)}, bf16[48,2048]{1,0:T(8,128)(2,1)}, u32[]{:S(2)}, u32[]{:S(2)}) collective-permute-start(bf16[48,2048]{1,0:T(8,128)(2,1)S(1)} %constant_dynamic-slice_fusion), channel_id=1, source_target_pairs={{2,0},{4,2},{6,4},{8,6},{10,8},{12,10},{14,12},{16,14},{18,16},{20... | collective-permute-start | bytes 589832 | tf_op jit(solution)/shard_map/ppermute | solution.py:46
  24.2 1.7 fusion.5
  26.2 2.0 collective-permute-start.2
  28.2 1.2 multiply_reduce_fusion
  29.9 1.3 collective-permute-start.3
  31.2 1.1 fusion.33
  32.9 2.2 collective-permute-done.3
  35.9 4.0 %all-to-all-start = ((f32[16,1,2176]{2,1,0:T(1,128)}), f32[16,1,2176]{2,1,0:T(1,128)S(1)}, u32[]{:S(2)}, u32[]{:S(2)}) async-start(f32[16,1,2176]{2,1,0:T(1,128)} %broadcast_in_dim.102), calls=%async_computation | async-start | bytes 278528 | tf_op jit(solution)/shard_map/all_to_all | solution.py:79
  39.9 1.5 collective-permute-start.9
  41.4 1.9 collective-permute-start.10
  43.2 0.9 bitcast_dynamic-update-slice_fusion.21
  44.2 0.9 bitcast_dynamic-update-slice_fusion.20
  45.1 7.7 %collective-permute-done.9 = bf16[48,2048]{1,0:T(8,128)(2,1)} collective-permute-done((bf16[48,2048]{1,0:T(8,128)(2,1)}, bf16[48,2048]{1,0:T(8,128)(2,1)}, u32[]{:S(2)}, u32[]{:S(2)}) %collective-permute-start.9) | collective-permute-done | bytes 196640 | tf_op jit(solution)/shard_map/ppermute | solution.py:44
  52.9 3.2 %collective-permute-start.12 = (bf16[48,2048]{1,0:T(8,128)(2,1)S(1)}, bf16[48,2048]{1,0:T(8,128)(2,1)}, u32[]{:S(2)}, u32[]{:S(2)}) collective-permute-start(bf16[48,2048]{1,0:T(8,128)(2,1)S(1)} %collective-permute-done.10), channel_id=1, source_target_pairs={{2,0},{4,2},{6,4},{8,6},{10,8},{12,10},{14,12},{16,14},{18,16},{20... | collective-permute-start | bytes 589832 | tf_op jit(solution)/shard_map/ppermute | solution.py:46
  56.1 0.9 bitcast_dynamic-update-slice_fusion.19
  57.2 1.5 collective-permute-start.4
  59.3 1.1 collective-permute-start.6
  61.9 1.7 collective-permute-done.5
  65.5 0.8 multiply_add_fusion
  67.0 2.2 fusion.9
  69.2 1.0 copy-done
  70.1 0.9 fusion.34
  71.0 0.9 copy.50
  71.9 9.8 %all-to-all-start.2 = ((bf16[64,16,256]{2,0,1:T(8,128)(2,1)}), bf16[64,16,256]{2,0,1:T(8,128)(2,1)}, u32[]{:S(2)}, u32[]{:S(2)}) async-start(bf16[64,16,256]{2,0,1:T(8,128)(2,1)} %bitcast.101), calls=%async_computation.2 | async-start | bytes 1048576 | tf_op jit(solution)/shard_map/all_to_all | solution.py:100
  81.7 1.8 collective-permute-start.13
  83.5 1.5 collective-permute-start.14
  85.0 0.9 bitcast_dynamic-update-slice_fusion.17
  86.0 0.9 bitcast_dynamic-update-slice_fusion.16
  86.9 22.4 %collective-permute-done.13 = bf16[48,2048]{1,0:T(8,128)(2,1)S(1)} collective-permute-done((bf16[48,2048]{1,0:T(8,128)(2,1)}, bf16[48,2048]{1,0:T(8,128)(2,1)S(1)}, u32[]{:S(2)}, u32[]{:S(2)}) %collective-permute-start.13) | collective-permute-done | bytes 196640 | tf_op jit(solution)/shard_map/ppermute | solution.py:44
  109.3 3.2 %collective-permute-start.16 = (bf16[48,2048]{1,0:T(8,128)(2,1)S(1)}, bf16[48,2048]{1,0:T(8,128)(2,1)S(1)}, u32[]{:S(2)}, u32[]{:S(2)}) collective-permute-start(bf16[48,2048]{1,0:T(8,128)(2,1)S(1)} %collective-permute-done.14), channel_id=1, source_target_pairs={{2,0},{4,2},{6,4},{8,6},{10,8},{12,10},{14,12},{16,14},{18,16},{20... | collective-permute-start | bytes 589832 | tf_op jit(solution)/shard_map/ppermute | solution.py:46
  112.6 3.6 %collective-permute-done.15 = bf16[48,2048]{1,0:T(8,128)(2,1)S(1)} collective-permute-done((bf16[48,2048]{1,0:T(8,128)(2,1)S(1)}, bf16[48,2048]{1,0:T(8,128)(2,1)S(1)}, u32[]{:S(2)}, u32[]{:S(2)}) %collective-permute-start.15) | collective-permute-done | bytes 196640 | tf_op jit(solution)/shard_map/ppermute | solution.py:44
  116.2 3.2 %collective-permute-start.18 = (bf16[48,2048]{1,0:T(8,128)(2,1)S(1)}, bf16[48,2048]{1,0:T(8,128)(2,1)S(1)}, u32[]{:S(2)}, u32[]{:S(2)}) collective-permute-start(bf16[48,2048]{1,0:T(8,128)(2,1)S(1)} %collective-permute-done.16), channel_id=1, source_target_pairs={{2,0},{4,2},{6,4},{8,6},{10,8},{12,10},{14,12},{16,14},{18,16},{20... | collective-permute-start | bytes 589832 | tf_op jit(solution)/shard_map/ppermute | solution.py:46
  119.5 3.6 %collective-permute-done.17 = bf16[48,2048]{1,0:T(8,128)(2,1)S(1)} collective-permute-done((bf16[48,2048]{1,0:T(8,128)(2,1)S(1)}, bf16[48,2048]{1,0:T(8,128)(2,1)S(1)}, u32[]{:S(2)}, u32[]{:S(2)}) %collective-permute-start.17) | collective-permute-done | bytes 196640 | tf_op jit(solution)/shard_map/ppermute | solution.py:44
  123.1 3.3 %collective-permute-start.20 = (bf16[48,2048]{1,0:T(8,128)(2,1)S(1)}, bf16[48,2048]{1,0:T(8,128)(2,1)S(1)}, u32[]{:S(2)}, u32[]{:S(2)}) collective-permute-start(bf16[48,2048]{1,0:T(8,128)(2,1)S(1)} %collective-permute-done.18), channel_id=1, source_target_pairs={{2,0},{4,2},{6,4},{8,6},{10,8},{12,10},{14,12},{16,14},{18,16},{20... | collective-permute-start | bytes 589832 | tf_op jit(solution)/shard_map/ppermute | solution.py:46
  126.4 4.5 %collective-permute-done.19 = bf16[48,2048]{1,0:T(8,128)(2,1)S(1)} collective-permute-done((bf16[48,2048]{1,0:T(8,128)(2,1)S(1)}, bf16[48,2048]{1,0:T(8,128)(2,1)S(1)}, u32[]{:S(2)}, u32[]{:S(2)}) %collective-permute-start.19) | collective-permute-done | bytes 196640 | tf_op jit(solution)/shard_map/ppermute | solution.py:44
  131.0 6.8 %collective-permute-done.21 = bf16[48,2048]{1,0:T(8,128)(2,1)S(1)} collective-permute-done((bf16[48,2048]{1,0:T(8,128)(2,1)S(1)}, bf16[48,2048]{1,0:T(8,128)(2,1)S(1)}, u32[]{:S(2)}, u32[]{:S(2)}) %collective-permute-start.21) | collective-permute-done | bytes 196640 | tf_op jit(solution)/shard_map/ppermute | solution.py:44
  138.0 2.4 collective-permute-start.22
  140.5 1.9 copy.51
  142.3 9.4 %all-to-all-start.1 = ((bf16[64,16,256]{2,0,1:T(8,128)(2,1)}), bf16[64,16,256]{2,0,1:T(8,128)(2,1)}, u32[]{:S(2)}, u32[]{:S(2)}) async-start(bf16[64,16,256]{2,0,1:T(8,128)(2,1)} %bitcast.102), calls=%async_computation.1 | async-start | bytes 1048576 | tf_op jit(solution)/shard_map/all_to_all | solution.py:100
  151.8 1.9 collective-permute-start.24
  153.8 1.1 constant_dynamic-update-slice_fusion
  154.9 1.1 bitcast_dynamic-update-slice_fusion.6
  156.0 1.1 bitcast_dynamic-update-slice_fusion.5
  157.1 10.3 %collective-permute-done.24 = bf16[1024,256]{1,0:T(8,128)(2,1)S(1)} collective-permute-done((bf16[1024,256]{1,0:T(8,128)(2,1)}, bf16[1024,256]{1,0:T(8,128)(2,1)S(1)}, u32[]{:S(2)}, u32[]{:S(2)}) %collective-permute-start.24) | collective-permute-done | bytes 524320 | tf_op jit(solution)/shard_map/ppermute | solution.py:16
  167.5 3.8 %fusion.3 = (bf16[768,2048]{1,0:T(8,128)(2,1)S(1)}, bf16[768,2048]{1,0:T(8,128)(2,1)S(1)}) fusion(bf16[16,48,2048]{2,1,0:T(8,128)(2,1)S(1)} %bitcast_dynamic-update-slice_fusion.7, f32[2048]{0:T(1024)S(1)} %get-tuple-element.44, f32[768]{0:T(1024)S(1)} %mul.118, f32[2048]{0:T(1024)S(1)} %get-tuple-element.45, bf16[16,48,2048]{2,1,0:T(8,128)(2,1)} %collective-permute-done.25), kind=kLoop, calls=%fused_computation.5 | loop fusion | flops 12582912 | bytes 12602368 | tf_op jit(solution)/shard_map/convert_element_type | solution.py:92
  171.3 1.6 copy-done.3
  172.9 1.0 fusion.15
  173.9 1.8 fusion.10
  175.7 5.2 %all-to-all-done.1 = bf16[64,16,256]{2,0,1:T(8,128)(2,1)} async-done(((bf16[64,16,256]{2,0,1:T(8,128)(2,1)}), bf16[64,16,256]{2,0,1:T(8,128)(2,1)}, u32[]{:S(2)}, u32[]{:S(2)}) %all-to-all-start.1) | async-done | bytes 524320 | tf_op jit(solution)/shard_map/all_to_all | solution.py:100
  180.8 3.1 %collective-permute-start.26 = (bf16[1024,256]{1,0:T(8,128)(2,1)}, bf16[1024,256]{1,0:T(8,128)(2,1)S(1)}, u32[]{:S(2)}, u32[]{:S(2)}) collective-permute-start(bf16[1024,256]{1,0:T(8,128)(2,1)} %bitcast.6), channel_id=1, source_target_pairs={{0,32},{32,64},{64,96},{96,0},{1,33},{33,65},{65,97},{97,1},{2,34}... | collective-permute-start | bytes 1572872 | tf_op jit(solution)/shard_map/ppermute | solution.py:16
  183.9 1.5 collective-permute-start.28
  185.4 6.5 %all-to-all-start.3 = ((bf16[16,48,256]{2,1,0:T(8,128)(2,1)}), bf16[16,48,256]{2,1,0:T(8,128)(2,1)S(1)}, u32[]{:S(2)}, u32[]{:S(2)}) async-start(bf16[16,48,256]{2,1,0:T(8,128)(2,1)} %bitcast.33), calls=%async_computation.3 | async-start | bytes 786432 | tf_op jit(solution)/shard_map/all_to_all | solution.py:109
  192.1 1.2 bitcast_dynamic-update-slice_fusion.3
  193.3 7.0 %collective-permute-done.26 = bf16[1024,256]{1,0:T(8,128)(2,1)S(1)} collective-permute-done((bf16[1024,256]{1,0:T(8,128)(2,1)}, bf16[1024,256]{1,0:T(8,128)(2,1)S(1)}, u32[]{:S(2)}, u32[]{:S(2)}) %collective-permute-start.26) | collective-permute-done | bytes 524320 | tf_op jit(solution)/shard_map/ppermute | solution.py:16
  200.4 3.2 %collective-permute-done.27 = bf16[1024,256]{1,0:T(8,128)(2,1)S(1)} collective-permute-done((bf16[1024,256]{1,0:T(8,128)(2,1)}, bf16[1024,256]{1,0:T(8,128)(2,1)S(1)}, u32[]{:S(2)}, u32[]{:S(2)}) %collective-permute-start.27) | collective-permute-done | bytes 524320 | tf_op jit(solution)/shard_map/ppermute | solution.py:16
  203.8 1.0 fusion.12
  204.7 0.8 copy-done.2
  205.6 1.7 fusion.11
  207.3 7.0 %all-to-all-done.3 = bf16[16,48,256]{2,1,0:T(8,128)(2,1)S(1)} async-done(((bf16[16,48,256]{2,1,0:T(8,128)(2,1)}), bf16[16,48,256]{2,1,0:T(8,128)(2,1)S(1)}, u32[]{:S(2)}, u32[]{:S(2)}) %all-to-all-start.3) | async-done | bytes 393248 | tf_op jit(solution)/shard_map/all_to_all | solution.py:109
  214.3 6.9 %all-to-all-start.4 = ((bf16[16,48,256]{2,1,0:T(8,128)(2,1)}), bf16[16,48,256]{2,1,0:T(8,128)(2,1)S(1)}, u32[]{:S(2)}, u32[]{:S(2)}) async-start(bf16[16,48,256]{2,1,0:T(8,128)(2,1)} %bitcast.40), calls=%async_computation.4 | async-start | bytes 786432 | tf_op jit(solution)/shard_map/all_to_all | solution.py:109
  221.4 23.0 %all-to-all-done.4 = bf16[16,48,256]{2,1,0:T(8,128)(2,1)S(1)} async-done(((bf16[16,48,256]{2,1,0:T(8,128)(2,1)}), bf16[16,48,256]{2,1,0:T(8,128)(2,1)S(1)}, u32[]{:S(2)}, u32[]{:S(2)}) %all-to-all-start.4) | async-done | bytes 393248 | tf_op jit(solution)/shard_map/all_to_all | solution.py:109
  245.1 0.9 pad_maximum_fusion
  (94 shorter events, 7.8 us)
Async XLA Ops:
  0.6 30.5 %copy-start.8 = (f32[64]{0:T(128)S(1)}, f32[64]{0:T(128)}, u32[]{:S(2)}) copy-start(f32[64]{0:T(128)} %param.13) | copy-start | bytes 772
  1.6 38.3 %collective-permute-start.7 = (bf16[48,2048]{1,0:T(8,128)(2,1)S(1)}, bf16[48,2048]{1,0:T(8,128)(2,1)}, u32[]{:S(2)}, u32[]{:S(2)}) collective-permute-start(bf16[48,2048]{1,0:T(8,128)(2,1)S(1)} %constant_dynamic-slice_fusion), channel_id=1, source_target_pairs={{0,2},{2,4},{4,6},{6,8},{8,10},{10,12},{12,14},{14,16},{16,18},{18... | collective-permute-start | bytes 589832 | tf_op jit(solution)/shard_map/ppermute | solution.py:44
  4.5 36.9 %collective-permute-start.8 = (bf16[48,2048]{1,0:T(8,128)(2,1)S(1)}, bf16[48,2048]{1,0:T(8,128)(2,1)}, u32[]{:S(2)}, u32[]{:S(2)}) collective-permute-start(bf16[48,2048]{1,0:T(8,128)(2,1)S(1)} %constant_dynamic-slice_fusion), channel_id=1, source_target_pairs={{2,0},{4,2},{6,4},{8,6},{10,8},{12,10},{14,12},{16,14},{18,16},{20... | collective-permute-start | bytes 589832 | tf_op jit(solution)/shard_map/ppermute | solution.py:46
  26.0 6.9 %collective-permute-start.1 = (f32[2048]{0:T(1024)S(1)}, f32[2048]{0:T(1024)S(1)}, u32[]{:S(2)}, u32[]{:S(2)}) collective-permute-start(f32[2048]{0:T(1024)S(1)} %bitcast.110), channel_id=1, source_target_pairs={{0,32},{32,64},{64,96},{96,0},{1,33},{33,65},{65,97},{97,1},{2,34}... | collective-permute-start | bytes 24584 | tf_op jit(solution)/shard_map/ppermute | solution.py:26
  26.2 6.7 %collective-permute-start.2 = (f32[2048]{0:T(1024)S(1)}, f32[2048]{0:T(1024)S(1)}, u32[]{:S(2)}, u32[]{:S(2)}) collective-permute-start(f32[2048]{0:T(1024)S(1)} %bitcast.109), channel_id=1, source_target_pairs={{0,96},{32,0},{64,32},{96,64},{1,97},{33,1},{65,33},{97,65},{2,98}... | collective-permute-start | bytes 24584 | tf_op jit(solution)/shard_map/ppermute | solution.py:26
  28.2 1.7 collective-permute-start
  29.9 5.3 %collective-permute-start.3 = (f32[2048]{0:T(1024)S(1)}, f32[2048]{0:T(1024)S(1)}, u32[]{:S(2)}, u32[]{:S(2)}) collective-permute-start(f32[2048]{0:T(1024)S(1)} %bitcast.108), channel_id=1, source_target_pairs={{0,64},{32,96},{64,0},{96,32},{1,65},{33,97},{65,1},{97,33},{2,66}... | collective-permute-start | bytes 24584 | tf_op jit(solution)/shard_map/ppermute | solution.py:26
  35.9 21.1 %all-to-all-start = ((f32[16,1,2176]{2,1,0:T(1,128)}), f32[16,1,2176]{2,1,0:T(1,128)S(1)}, u32[]{:S(2)}, u32[]{:S(2)}) async-start(f32[16,1,2176]{2,1,0:T(1,128)} %broadcast_in_dim.102), calls=%async_computation | async-start | bytes 278528 | tf_op jit(solution)/shard_map/all_to_all | solution.py:79
  39.9 13.0 %collective-permute-start.9 = (bf16[48,2048]{1,0:T(8,128)(2,1)}, bf16[48,2048]{1,0:T(8,128)(2,1)}, u32[]{:S(2)}, u32[]{:S(2)}) collective-permute-start(bf16[48,2048]{1,0:T(8,128)(2,1)} %collective-permute-done.7), channel_id=1, source_target_pairs={{0,2},{2,4},{4,6},{6,8},{8,10},{10,12},{12,14},{14,16},{16,18},{18... | collective-permute-start | bytes 589832 | tf_op jit(solution)/shard_map/ppermute | solution.py:44
  41.4 11.5 %collective-permute-start.10 = (bf16[48,2048]{1,0:T(8,128)(2,1)}, bf16[48,2048]{1,0:T(8,128)(2,1)S(1)}, u32[]{:S(2)}, u32[]{:S(2)}) collective-permute-start(bf16[48,2048]{1,0:T(8,128)(2,1)} %collective-permute-done.8), channel_id=1, source_target_pairs={{2,0},{4,2},{6,4},{8,6},{10,8},{12,10},{14,12},{16,14},{18,16},{20... | collective-permute-start | bytes 589832 | tf_op jit(solution)/shard_map/ppermute | solution.py:46
  52.9 28.8 %collective-permute-start.11 = (bf16[48,2048]{1,0:T(8,128)(2,1)}, bf16[48,2048]{1,0:T(8,128)(2,1)}, u32[]{:S(2)}, u32[]{:S(2)}) collective-permute-start(bf16[48,2048]{1,0:T(8,128)(2,1)} %collective-permute-done.9), channel_id=1, source_target_pairs={{0,2},{2,4},{4,6},{6,8},{8,10},{10,12},{12,14},{14,16},{16,18},{18... | collective-permute-start | bytes 589832 | tf_op jit(solution)/shard_map/ppermute | solution.py:44
  52.9 30.6 %collective-permute-start.12 = (bf16[48,2048]{1,0:T(8,128)(2,1)S(1)}, bf16[48,2048]{1,0:T(8,128)(2,1)}, u32[]{:S(2)}, u32[]{:S(2)}) collective-permute-start(bf16[48,2048]{1,0:T(8,128)(2,1)S(1)} %collective-permute-done.10), channel_id=1, source_target_pairs={{2,0},{4,2},{6,4},{8,6},{10,8},{12,10},{14,12},{16,14},{18,16},{20... | collective-permute-start | bytes 589832 | tf_op jit(solution)/shard_map/ppermute | solution.py:46
  57.2 3.9 %collective-permute-start.4 = (f32[2176]{0:T(1024)S(1)}, f32[2176]{0:T(1024)}, u32[]{:S(2)}, u32[]{:S(2)}) collective-permute-start(f32[2176]{0:T(1024)S(1)} %reduce_sum.58), channel_id=1, source_target_pairs={{0,32},{32,64},{64,96},{96,0},{1,33},{33,65},{65,97},{97,1},{2,34}... | collective-permute-start | bytes 26120 | tf_op jit(solution)/shard_map/ppermute | solution.py:16
  58.6 5.0 %collective-permute-start.5 = (f32[2176]{0:T(1024)S(1)}, f32[2176]{0:T(1024)}, u32[]{:S(2)}, u32[]{:S(2)}) collective-permute-start(f32[2176]{0:T(1024)S(1)} %reduce_sum.58), channel_id=1, source_target_pairs={{0,96},{32,0},{64,32},{96,64},{1,97},{33,1},{65,33},{97,65},{2,98}... | collective-permute-start | bytes 26120 | tf_op jit(solution)/shard_map/ppermute | solution.py:16
  59.3 5.2 %collective-permute-start.6 = (f32[2176]{0:T(1024)S(1)}, f32[2176]{0:T(1024)S(1)}, u32[]{:S(2)}, u32[]{:S(2)}) collective-permute-start(f32[2176]{0:T(1024)S(1)} %reduce_sum.58), channel_id=1, source_target_pairs={{0,64},{32,96},{64,0},{96,32},{1,65},{33,97},{65,1},{97,33},{2,66}... | collective-permute-start | bytes 26120 | tf_op jit(solution)/shard_map/ppermute | solution.py:16
  66.3 5.6 %copy-start.6 = (f32[8192]{0:T(1024)}, f32[8192]{0:T(1024)S(1)}, u32[]{:S(2)}) copy-start(f32[8192]{0:T(1024)S(1)} %multiply_add_fusion) | copy-start | bytes 98308
  69.2 1.0 copy-start
  71.0 69.3 %copy-start.7 = (bf16[4096]{0:T(1024)(128)(2,1)S(1)}, bf16[4096]{0:T(1024)(128)(2,1)}, u32[]{:S(2)}) copy-start(bf16[4096]{0:T(1024)(128)(2,1)} %param.16) | copy-start | bytes 24580
  71.9 66.1 %all-to-all-start.2 = ((bf16[64,16,256]{2,0,1:T(8,128)(2,1)}), bf16[64,16,256]{2,0,1:T(8,128)(2,1)}, u32[]{:S(2)}, u32[]{:S(2)}) async-start(bf16[64,16,256]{2,0,1:T(8,128)(2,1)} %bitcast.101), calls=%async_computation.2 | async-start | bytes 1048576 | tf_op jit(solution)/shard_map/all_to_all | solution.py:100
  81.7 27.6 %collective-permute-start.13 = (bf16[48,2048]{1,0:T(8,128)(2,1)}, bf16[48,2048]{1,0:T(8,128)(2,1)S(1)}, u32[]{:S(2)}, u32[]{:S(2)}) collective-permute-start(bf16[48,2048]{1,0:T(8,128)(2,1)} %collective-permute-done.11), channel_id=1, source_target_pairs={{0,2},{2,4},{4,6},{6,8},{8,10},{10,12},{12,14},{14,16},{16,18},{18... | collective-permute-start | bytes 589832 | tf_op jit(solution)/shard_map/ppermute | solution.py:44
  83.5 25.8 %collective-permute-start.14 = (bf16[48,2048]{1,0:T(8,128)(2,1)}, bf16[48,2048]{1,0:T(8,128)(2,1)S(1)}, u32[]{:S(2)}, u32[]{:S(2)}) collective-permute-start(bf16[48,2048]{1,0:T(8,128)(2,1)} %collective-permute-done.12), channel_id=1, source_target_pairs={{2,0},{4,2},{6,4},{8,6},{10,8},{12,10},{14,12},{16,14},{18,16},{20... | collective-permute-start | bytes 589832 | tf_op jit(solution)/shard_map/ppermute | solution.py:46
  109.3 6.9 %collective-permute-start.15 = (bf16[48,2048]{1,0:T(8,128)(2,1)S(1)}, bf16[48,2048]{1,0:T(8,128)(2,1)S(1)}, u32[]{:S(2)}, u32[]{:S(2)}) collective-permute-start(bf16[48,2048]{1,0:T(8,128)(2,1)S(1)} %collective-permute-done.13), channel_id=1, source_target_pairs={{0,2},{2,4},{4,6},{6,8},{8,10},{10,12},{12,14},{14,16},{16,18},{18... | collective-permute-start | bytes 589832 | tf_op jit(solution)/shard_map/ppermute | solution.py:44
  109.3 6.9 %collective-permute-start.16 = (bf16[48,2048]{1,0:T(8,128)(2,1)S(1)}, bf16[48,2048]{1,0:T(8,128)(2,1)S(1)}, u32[]{:S(2)}, u32[]{:S(2)}) collective-permute-start(bf16[48,2048]{1,0:T(8,128)(2,1)S(1)} %collective-permute-done.14), channel_id=1, source_target_pairs={{2,0},{4,2},{6,4},{8,6},{10,8},{12,10},{14,12},{16,14},{18,16},{20... | collective-permute-start | bytes 589832 | tf_op jit(solution)/shard_map/ppermute | solution.py:46
  116.2 6.9 %collective-permute-start.17 = (bf16[48,2048]{1,0:T(8,128)(2,1)S(1)}, bf16[48,2048]{1,0:T(8,128)(2,1)S(1)}, u32[]{:S(2)}, u32[]{:S(2)}) collective-permute-start(bf16[48,2048]{1,0:T(8,128)(2,1)S(1)} %collective-permute-done.15), channel_id=1, source_target_pairs={{0,2},{2,4},{4,6},{6,8},{8,10},{10,12},{12,14},{14,16},{16,18},{18... | collective-permute-start | bytes 589832 | tf_op jit(solution)/shard_map/ppermute | solution.py:44
  116.2 6.9 %collective-permute-start.18 = (bf16[48,2048]{1,0:T(8,128)(2,1)S(1)}, bf16[48,2048]{1,0:T(8,128)(2,1)S(1)}, u32[]{:S(2)}, u32[]{:S(2)}) collective-permute-start(bf16[48,2048]{1,0:T(8,128)(2,1)S(1)} %collective-permute-done.16), channel_id=1, source_target_pairs={{2,0},{4,2},{6,4},{8,6},{10,8},{12,10},{14,12},{16,14},{18,16},{20... | collective-permute-start | bytes 589832 | tf_op jit(solution)/shard_map/ppermute | solution.py:46
  123.0 7.9 %collective-permute-start.19 = (bf16[48,2048]{1,0:T(8,128)(2,1)S(1)}, bf16[48,2048]{1,0:T(8,128)(2,1)S(1)}, u32[]{:S(2)}, u32[]{:S(2)}) collective-permute-start(bf16[48,2048]{1,0:T(8,128)(2,1)S(1)} %collective-permute-done.17), channel_id=1, source_target_pairs={{0,2},{2,4},{4,6},{6,8},{8,10},{10,12},{12,14},{14,16},{16,18},{18... | collective-permute-start | bytes 589832 | tf_op jit(solution)/shard_map/ppermute | solution.py:44
  123.1 7.9 %collective-permute-start.20 = (bf16[48,2048]{1,0:T(8,128)(2,1)S(1)}, bf16[48,2048]{1,0:T(8,128)(2,1)S(1)}, u32[]{:S(2)}, u32[]{:S(2)}) collective-permute-start(bf16[48,2048]{1,0:T(8,128)(2,1)S(1)} %collective-permute-done.18), channel_id=1, source_target_pairs={{2,0},{4,2},{6,4},{8,6},{10,8},{12,10},{14,12},{16,14},{18,16},{20... | collective-permute-start | bytes 589832 | tf_op jit(solution)/shard_map/ppermute | solution.py:46
  130.9 6.9 %collective-permute-start.21 = (bf16[48,2048]{1,0:T(8,128)(2,1)S(1)}, bf16[48,2048]{1,0:T(8,128)(2,1)S(1)}, u32[]{:S(2)}, u32[]{:S(2)}) collective-permute-start(bf16[48,2048]{1,0:T(8,128)(2,1)S(1)} %collective-permute-done.19), channel_id=1, source_target_pairs={{0,2},{2,4},{4,6},{6,8},{8,10},{10,12},{12,14},{14,16},{16,18},{18... | collective-permute-start | bytes 589832 | tf_op jit(solution)/shard_map/ppermute | solution.py:44
  137.8 29.7 %collective-permute-start.25 = (bf16[16,48,2048]{2,1,0:T(8,128)(2,1)S(1)}, bf16[16,48,2048]{2,1,0:T(8,128)(2,1)}, u32[]{:S(2)}, u32[]{:S(2)}) collective-permute-start(bf16[16,48,2048]{2,1,0:T(8,128)(2,1)S(1)} %bitcast_dynamic-update-slice_fusion.7), channel_id=1, source_target_pairs={{0,1},{1,0},{2,3},{3,2},{4,5},{5,4},{6,7},{7,6},{8,9},{9,8},{10,11... | collective-permute-start | bytes 9437192 | tf_op jit(solution)/shard_map/ppermute | solution.py:65
  138.0 17.0 %collective-permute-start.22 = (bf16[1024,256]{1,0:T(8,128)(2,1)}, bf16[1024,256]{1,0:T(8,128)(2,1)}, u32[]{:S(2)}, u32[]{:S(2)}) collective-permute-start(bf16[1024,256]{1,0:T(8,128)(2,1)} %bitcast.26), channel_id=1, source_target_pairs={{0,32},{32,64},{64,96},{96,0},{1,33},{33,65},{65,97},{97,1},{2,34}... | collective-permute-start | bytes 1572872 | tf_op jit(solution)/shard_map/ppermute | solution.py:16
  140.3 15.7 %collective-permute-start.23 = (bf16[1024,256]{1,0:T(8,128)(2,1)}, bf16[1024,256]{1,0:T(8,128)(2,1)}, u32[]{:S(2)}, u32[]{:S(2)}) collective-permute-start(bf16[1024,256]{1,0:T(8,128)(2,1)} %bitcast.26), channel_id=1, source_target_pairs={{0,96},{32,0},{64,32},{96,64},{1,97},{33,1},{65,33},{97,65},{2,98}... | collective-permute-start | bytes 1572872 | tf_op jit(solution)/shard_map/ppermute | solution.py:16
  142.3 38.5 %all-to-all-start.1 = ((bf16[64,16,256]{2,0,1:T(8,128)(2,1)}), bf16[64,16,256]{2,0,1:T(8,128)(2,1)}, u32[]{:S(2)}, u32[]{:S(2)}) async-start(bf16[64,16,256]{2,0,1:T(8,128)(2,1)} %bitcast.102), calls=%async_computation.1 | async-start | bytes 1048576 | tf_op jit(solution)/shard_map/all_to_all | solution.py:100
  151.8 15.7 %collective-permute-start.24 = (bf16[1024,256]{1,0:T(8,128)(2,1)}, bf16[1024,256]{1,0:T(8,128)(2,1)S(1)}, u32[]{:S(2)}, u32[]{:S(2)}) collective-permute-start(bf16[1024,256]{1,0:T(8,128)(2,1)} %bitcast.26), channel_id=1, source_target_pairs={{0,64},{32,96},{64,0},{96,32},{1,65},{33,97},{65,1},{97,33},{2,66}... | collective-permute-start | bytes 1572872 | tf_op jit(solution)/shard_map/ppermute | solution.py:16
  171.3 1.6 copy-start.3
  171.3 2.6 %copy-start.1 = (bf16[768,2048]{1,0:T(8,128)(2,1)}, bf16[768,2048]{1,0:T(8,128)(2,1)S(1)}, u32[]{:S(2)}) copy-start(bf16[768,2048]{1,0:T(8,128)(2,1)S(1)} %get-tuple-element.46) | copy-start | bytes 9437188
  180.8 19.5 %collective-permute-start.26 = (bf16[1024,256]{1,0:T(8,128)(2,1)}, bf16[1024,256]{1,0:T(8,128)(2,1)S(1)}, u32[]{:S(2)}, u32[]{:S(2)}) collective-permute-start(bf16[1024,256]{1,0:T(8,128)(2,1)} %bitcast.6), channel_id=1, source_target_pairs={{0,32},{32,64},{64,96},{96,0},{1,33},{33,65},{65,97},{97,1},{2,34}... | collective-permute-start | bytes 1572872 | tf_op jit(solution)/shard_map/ppermute | solution.py:16
  183.9 19.7 %collective-permute-start.27 = (bf16[1024,256]{1,0:T(8,128)(2,1)}, bf16[1024,256]{1,0:T(8,128)(2,1)S(1)}, u32[]{:S(2)}, u32[]{:S(2)}) collective-permute-start(bf16[1024,256]{1,0:T(8,128)(2,1)} %bitcast.6), channel_id=1, source_target_pairs={{0,96},{32,0},{64,32},{96,64},{1,97},{33,1},{65,33},{97,65},{2,98}... | collective-permute-start | bytes 1572872 | tf_op jit(solution)/shard_map/ppermute | solution.py:16
  183.9 19.7 %collective-permute-start.28 = (bf16[1024,256]{1,0:T(8,128)(2,1)}, bf16[1024,256]{1,0:T(8,128)(2,1)S(1)}, u32[]{:S(2)}, u32[]{:S(2)}) collective-permute-start(bf16[1024,256]{1,0:T(8,128)(2,1)} %bitcast.6), channel_id=1, source_target_pairs={{0,64},{32,96},{64,0},{96,32},{1,65},{33,97},{65,1},{97,33},{2,66}... | collective-permute-start | bytes 1572872 | tf_op jit(solution)/shard_map/ppermute | solution.py:16
  185.4 28.9 %all-to-all-start.3 = ((bf16[16,48,256]{2,1,0:T(8,128)(2,1)}), bf16[16,48,256]{2,1,0:T(8,128)(2,1)S(1)}, u32[]{:S(2)}, u32[]{:S(2)}) async-start(bf16[16,48,256]{2,1,0:T(8,128)(2,1)} %bitcast.33), calls=%async_computation.3 | async-start | bytes 786432 | tf_op jit(solution)/shard_map/all_to_all | solution.py:109
  191.9 11.8 %copy-start.4 = (bf16[768,2048]{1,0:T(8,128)(2,1)S(1)}, bf16[768,2048]{1,0:T(8,128)(2,1)}, u32[]{:S(2)}) copy-start(bf16[768,2048]{1,0:T(8,128)(2,1)} %copy-done.3) | copy-start | bytes 9437188
  203.7 1.9 copy-start.2
  214.3 30.3 %copy-start.5 = (bf16[48,8192]{1,0:T(8,128)(2,1)S(1)}, bf16[48,8192]{1,0:T(8,128)(2,1)}, u32[]{:S(2)}) copy-start(bf16[48,8192]{1,0:T(8,128)(2,1)} %param.17) | copy-start | bytes 2359300
  214.3 30.1 %all-to-all-start.4 = ((bf16[16,48,256]{2,1,0:T(8,128)(2,1)}), bf16[16,48,256]{2,1,0:T(8,128)(2,1)S(1)}, u32[]{:S(2)}, u32[]{:S(2)}) async-start(bf16[16,48,256]{2,1,0:T(8,128)(2,1)} %bitcast.40), calls=%async_computation.4 | async-start | bytes 786432 | tf_op jit(solution)/shard_map/all_to_all | solution.py:109

commit v2 on v0

v2 whole, which is shorter than its diff:
```python
import jax
import jax.numpy as jnp
from jax import lax
from jax.experimental import pallas as pl
from jax.experimental.pallas import tpu as pltpu
from jax.sharding import Mesh
from jax.sharding import PartitionSpec as P

JOB_FSDP = ("job", "fsdp_0", "fsdp_1")
X, Z = "fsdp_0", "fsdp_1"
CHUNKS = 2
LANES = 128
VMEM_LIMIT = 16 * 2**20


def steps(size):
    return sorted(range(size), key=lambda k: min(k, size - k))


def shifted(x, axis, step):
    size = lax.axis_size(axis)
    return x if step == 0 else lax.ppermute(x, axis, [(i, (i + step) % size) for i in range(size)])


def scatter_sum(x, axis):
    size, me = lax.axis_size(axis), lax.axis_index(axis)
    blocks = x.reshape(size, -1, x.shape[1])
    total = 0
    for step in steps(size):
        block = lax.dynamic_index_in_dim(blocks, lax.rem(me + step, size), 0, keepdims=False)
        total += shifted(block, axis, step)
    return total


def dot(a, b):
    return jnp.dot(a, b, preferred_element_type=jnp.float32)


def vmem(n):
    return [pl.BlockSpec(memory_space=pltpu.VMEM)] * n


def apply_update(pieces, me, col_moment, new_rows, grad, weight, n_z, rows):
    size, local_rows, local_columns = len(pieces), *grad.shape
    share = col_moment.shape[0] // size
    width = local_columns // CHUNKS // n_z

    def kernel(me_ref, *refs):
        piece_refs, refs = refs[:size], refs[size:]
        moment_ref, rows_ref, grad_ref, weight_ref, out_ref, columns_ref, *send_refs, factor_ref = refs
        rows_summed = 0.0
        for step, piece_ref in zip(steps(size), piece_refs, strict=True):
            source = lax.rem(me_ref[0] - step + size, size)
            place = pl.ds(pl.multiple_of(source * share, share), share)
            factor_ref[place, :] = piece_ref[:share, :]
            rows_summed += piece_ref[share : share + 1, LANES - 1 :]
        new_columns = 0.8 * moment_ref[...] + 0.2 * (factor_ref[...] / rows)
        columns_ref[...] = new_columns
        factor_ref[...] = 0.01 * jnp.sqrt((rows_summed / rows) / new_columns)
        row_factor = jnp.broadcast_to(1.0 / jnp.sqrt(rows_ref[...]), (local_rows, LANES))
        for group in range(local_columns // LANES):
            at = group * LANES
            part = slice(at, at + LANES)
            scaled = grad_ref[:, part].astype(jnp.float32) * row_factor * factor_ref[group : group + 1, :]
            new = (weight_ref[:, part].astype(jnp.float32) - scaled).astype(jnp.bfloat16)
            out_ref[:, part] = new
            chunk, rest = divmod(at, width * n_z)
            target, rest = divmod(rest, width)
            send_refs[chunk][target, :, rest : rest + LANES] = new

    send = jax.ShapeDtypeStruct((n_z, local_rows, width), jnp.bfloat16)
    return pl.pallas_call(
        kernel,
        out_shape=[
            jax.ShapeDtypeStruct(grad.shape, jnp.bfloat16),
            jax.ShapeDtypeStruct(col_moment.shape, jnp.float32),
            *[send] * CHUNKS,
        ],
        in_specs=[pl.BlockSpec(memory_space=pltpu.SMEM), *vmem(size + 4)],
        out_specs=vmem(2 + CHUNKS),
        scratch_shapes=[pltpu.VMEM(col_moment.shape, jnp.float32)],
        compiler_params=pltpu.CompilerParams(vmem_limit_bytes=VMEM_LIMIT),
    )(me.reshape(1), *pieces, col_moment, new_rows.reshape(-1, 1), grad, weight)


def finish(up, gate, hidden, chunk):
    n_z, tokens, width = up.shape

    def kernel(up_ref, gate_ref, *refs):
        out_ref = refs[-1]
        for z in range(n_z):
            part = slice(z * width, (z + 1) * width)
            v = gate_ref[:, part].astype(jnp.float32)
            out_ref[:, part] = (v / (1.0 + jnp.exp(-v)) * up_ref[z].astype(jnp.float32)).astype(jnp.bfloat16)

    block = pl.BlockSpec((tokens, n_z * width), lambda i: (0, chunk))
    first = hidden is None
    return pl.pallas_call(
        kernel,
        grid=(1,),
        out_shape=jax.ShapeDtypeStruct(gate.shape, jnp.bfloat16),
        in_specs=[pl.BlockSpec(up.shape, lambda i: (0, 0, 0)), block]
        + ([] if first else [pl.BlockSpec(memory_space=pl.ANY)]),
        out_specs=block,
        input_output_aliases={} if first else {2: 0},
        compiler_params=pltpu.CompilerParams(vmem_limit_bytes=VMEM_LIMIT),
    )(up, gate, *([] if first else [hidden]))


def step(weight, grad, row_moment, col_moment, states, norm_gain, gate_values):
    n_x, n_z, n_tp = lax.axis_size(X), lax.axis_size(Z), lax.axis_size("tp")
    me_x, me_tp = lax.axis_index(X), lax.axis_index("tp")
    local_rows, local_columns = grad.shape
    columns = local_columns * n_tp
    rows = local_rows * n_x * n_z
    values = states.astype(jnp.float32)
    scale = lax.rsqrt(jnp.mean(values * values, axis=1) + 1e-06)

    features = states.shape[1]
    share, piece = features // n_tp, features // n_x
    tokens = lax.dynamic_slice_in_dim(states, me_tp * share, share, 1)
    tokens = lax.all_gather(tokens, Z, axis=0, tiled=True)
    other_tokens = lax.ppermute(tokens, "tp", [(0, 1), (1, 0)])

    gradient = grad.astype(jnp.float32)
    squares = gradient * gradient + 1e-30
    row_partial = jnp.sum(squares, axis=1)
    col_partial = jnp.sum(squares, axis=0).reshape(-1, LANES)
    row_total = row_partial + lax.ppermute(row_partial, "tp", [(0, 1), (1, 0)])
    new_rows = 0.8 * row_moment + 0.2 * (row_total / columns)
    quarter = scatter_sum(col_partial, X)
    n_quarter = quarter.shape[0]
    extra = jnp.concatenate([scale, jnp.zeros((LANES - 1 - scale.shape[0],), jnp.float32), jnp.sum(new_rows).reshape(1)])
    mine = jnp.concatenate([quarter, jnp.broadcast_to(extra, (8, LANES))])
    theirs = lax.all_to_all(jnp.broadcast_to(mine, (n_z, *mine.shape)), Z, 0, 0)
    scales = theirs[:, n_quarter, : scale.shape[0]].reshape(-1, 1)
    mine = theirs.sum(axis=0)
    pieces = [shifted(mine, X, k) for k in steps(n_x)]
    new_weight, new_columns, *sends = apply_update(
        pieces, me_x, col_moment.reshape(-1, LANES), new_rows, grad, weight, n_z, rows
    )

    normed = jnp.zeros((n_x, tokens.shape[0], piece), jnp.bfloat16)
    for part, half in ((tokens, me_tp), (other_tokens, n_tp - 1 - me_tp)):
        gain = lax.dynamic_slice_in_dim(norm_gain, half * share, share, 0).astype(jnp.float32)
        part = (part.astype(jnp.float32) * scales * gain).astype(jnp.bfloat16)
        for i in range(share // piece):
            block = part[:, i * piece : (i + 1) * piece]
            normed = lax.dynamic_update_index_in_dim(normed, block, half * (share // piece) + i, 0)
    normed = lax.optimization_barrier(normed)

    ups = []
    for send in sends:
        block = lax.all_to_all(send, Z, 0, 0).reshape(-1, send.shape[2])
        if ups:
            block, ups[-1] = lax.optimization_barrier((block, ups[-1]))
        up = 0
        for k in steps(n_x):
            moved = shifted(block, X, k)
            source = lax.rem(me_x - k + n_x, n_x)
            up += dot(lax.dynamic_index_in_dim(normed, source, 0, keepdims=False), moved)
        ups.append(up.astype(jnp.bfloat16))
    hidden = None
    for c, up in enumerate(ups):
        up = lax.all_to_all(up.reshape(n_z, -1, up.shape[1]), Z, 0, 0)
        hidden = finish(up, gate_values, hidden, c)
    return (new_weight, new_rows, new_columns.reshape(-1), hidden)


def solution(mesh):
    job, fsdp, tp = (mesh.shape[n] for n in ("job", "fsdp", "tp"))
    finer = Mesh(mesh.devices.reshape(job, 4, fsdp // 4, tp), ("job", X, Z, "tp"))
    placed = (
        P(JOB_FSDP, "tp"),
        P(JOB_FSDP, "tp"),
        P(JOB_FSDP),
        P(("job", "tp")),
        P(JOB_FSDP, None),
        P("job"),
        P(JOB_FSDP, "tp"),
    )
    return jax.shard_map(
        step,
        mesh=finer,
        in_specs=placed,
        out_specs=(P(JOB_FSDP, "tp"), P(JOB_FSDP), P(("job", "tp")), P(JOB_FSDP, "tp")),
        check_vma=False,
    )
```

time: 238 us -> 284 us (1.19)
  waiting for transfers between devices: 115 us -> 162 us
  blocking collectives: 39.2 us -> 23.5 us
  starting transfers between devices: 43.3 us -> 49.9 us
  Pallas kernels: 0 us -> 3.7 us
  matrix products: 9.56 us -> 12.9 us
  local copies, waits for them, and re-layouts: 3.42 us -> 6.75 us
    all_gather x1, waiting for transfers between devices: 46.9 us -> 80.4 us  [step(): tokens = lax.all_gather(tokens, Z, axis=0, tiled=True)]
    all_to_all x1, blocking collectives: 39.2 us -> 23.5 us  [step(): theirs = lax.all_to_all(jnp.broadcast_to(mine, (n_z, *mine.shape)), Z, 0, 0)]
    all_to_all x4, waiting for transfers between devices: 28.3 us -> 42.4 us  [the longest x2 26.5 us: step(): block = lax.all_to_all(send, Z, 0, 0).reshape(-1, send.shape[2])]
    all_to_all x4, starting transfers between devices: 31 us -> 37 us  [the longest x2 23.3 us: step(): up = lax.all_to_all(up.reshape(n_z, -1, up.shape[1]), Z, 0, 0)]
    pallas_call x0 -> x3, Pallas kernels: none -> 3.7 us  [the longest x2 2 us: finish(): pl.pallas_call(kernel, grid=(1,), out_shape=jax.ShapeDtypeStruct(gate.sha...]
    dot_general x4 -> x8, matrix products: 9.56 us -> 12.9 us  [dot(): return jnp.dot(a, b, preferred_element_type=jnp.float32)]
    unnamed x21 -> x16, local copies, waits for them, and re-layouts: 0.05 us -> 3.23 us
  transfers between devices with their start and end apart: 19 -> 19, of which waited for: 12 -> 9; matrix products, arithmetic and copies ran while one was open for 6% -> 8% of each run, Pallas kernels for 0% -> 1%
where the time goes in v2:
time: 284 us; the launch traced here: 282 us
  waiting for transfers between devices  162 us (57%)
  starting transfers between devices  49.9 us (18%)
  blocking collectives  23.5 us (8%)
  between operations  14.4 us (5%)
  matrix products  12.9 us (5%)
  other arithmetic  8.54 us (3%)
  local copies, waits for them, and re-layouts  6.75 us (2%)
  Pallas kernels  3.7 us (1%)
    all_gather x1, waiting for transfers between devices, step(): tokens = lax.all_gather(tokens, Z, axis=0, tiled=True)  80.4 us
    ppermute x12, waiting for transfers between devices, shifted(): lax.ppermute(x, axis, [(i, (i + step) % size) for i in range(size)])  39.3 us
    all_to_all x2, waiting for transfers between devices, step(): block = lax.all_to_all(send, Z, 0, 0).reshape(-1, send.shape[2])  26.5 us
    all_to_all x1, blocking collectives, step(): theirs = lax.all_to_all(jnp.broadcast_to(mine, (n_z, *mine.shape)), Z, 0, 0)  23.5 us
    all_to_all x2, starting transfers between devices, step(): up = lax.all_to_all(up.reshape(n_z, -1, up.shape[1]), Z, 0, 0)  23.3 us
    all_to_all x2, waiting for transfers between devices, step(): up = lax.all_to_all(up.reshape(n_z, -1, up.shape[1]), Z, 0, 0)  15.9 us
    all_to_all x2, starting transfers between devices, step(): block = lax.all_to_all(send, Z, 0, 0).reshape(-1, send.shape[2])  13.7 us
    dot_general x8, matrix products, dot(): return jnp.dot(a, b, preferred_element_type=jnp.float32)  12.9 us
  transfers between devices with their start and end apart: 19, of which 9 were waited for; matrix products, arithmetic and copies ran while one was open for 8% of the time, Pallas kernels for 1%

profile of v2, /device:TPU:46, one launch (start us, length us, event | category | flops | bytes accessed | tf_op | source)
XLA Modules:
  0.0 281.9 jit_solution(11706968807027453225)
XLA Ops:
  7.2 0.1 all-gather.2.cloned.1.call-start
  7.3 1.6 constant_dynamic-slice_fusion
  8.9 0.1 all-gather.2.cloned.1.call-update
  9.0 1.7 fusion.1
  10.7 0.2 collective-permute-start
  10.9 2.0 collective-permute-start.1
  12.9 1.1 collective-permute-start.2
  14.0 0.0 collective-permute-start.3
  14.0 1.2 multiply_reduce_fusion
  15.2 0.0 collective-permute-done.3
  15.2 1.3 fusion.64
  16.5 80.4 %all-gather.2.cloned.1.call-done = bf16[768,2048]{1,0:T(8,128)(2,1)} async-done(((bf16[48,2048]{1,0:T(8,128)(2,1)}), bf16[768,2048]{1,0:T(8,128)(2,1)}) %all-gather.2.cloned.1.call-update) | async-done | bytes 3145744 | tf_op jit(solution)/shard_map/all_gather | solution.py:122
  96.9 0.0 collective-permute-start.7
  96.9 0.7 pad_maximum_fusion.1
  97.6 0.0 collective-permute-done
  97.7 23.5 %all_to_all.25 = f32[16,24,128]{2,1,0:T(8,128)S(1)} all-to-all(f32[16,24,128]{2,1,0:T(8,128)S(1)} %broadcast_in_dim.29), channel_id=1, replica_groups=mesh['job'=2,'fsdp_0'=4,'fsdp_1'=16,'tp'=2] {'fsdp_1'}, dimensions={0} | all-to-all | bytes 393216 | tf_op jit(solution)/shard_map/all_to_all | solution.py:135
  121.2 0.6 collective-permute-start.4
  121.9 1.5 collective-permute-start.5
  123.4 1.4 collective-permute-start.6
  124.8 0.1 copy.13.refs_5_
  124.9 0.1 collective-permute-done.4.refs_1_
  125.1 1.7 collective-permute-done.5.refs_2_
  126.8 1.8 collective-permute-done.6.refs_3_
  128.6 1.2 copy-done
  129.8 1.2 copy-done.2
  131.0 0.8 copy-done.3
  131.8 1.7 shard_map.102
  133.5 6.4 %all-to-all-start.2 = ((bf16[16,64,256]{2,1,0:T(8,128)(2,1)}), bf16[16,64,256]{2,1,0:T(8,128)(2,1)}, u32[]{:S(2)}, u32[]{:S(2)}) async-start(bf16[16,64,256]{2,1,0:T(8,128)(2,1)} %get-tuple-element.13), calls=%async_computation.2 | async-start | bytes 1048576 | tf_op jit(solution)/shard_map/all_to_all | solution.py:154
  140.0 0.1 mul.72
  140.1 26.5 %all-to-all-done.2 = bf16[16,64,256]{2,1,0:T(8,128)(2,1)} async-done(((bf16[16,64,256]{2,1,0:T(8,128)(2,1)}), bf16[16,64,256]{2,1,0:T(8,128)(2,1)}, u32[]{:S(2)}, u32[]{:S(2)}) %all-to-all-start.2) | async-done | bytes 524320 | tf_op jit(solution)/shard_map/all_to_all | solution.py:154
  166.6 7.3 %all-to-all-start.1 = ((bf16[16,64,256]{2,1,0:T(8,128)(2,1)}), bf16[16,64,256]{2,1,0:T(8,128)(2,1)}, u32[]{:S(2)}, u32[]{:S(2)}) async-start(bf16[16,64,256]{2,1,0:T(8,128)(2,1)} %get-tuple-element.12), calls=%async_computation.1 | async-start | bytes 1048576 | tf_op jit(solution)/shard_map/all_to_all | solution.py:154
  173.8 1.9 collective-permute-start.8
  175.7 0.3 collective-permute-start.9
  176.0 1.4 collective-permute-start.10
  177.4 3.6 %multiply_convert_fusion = (bf16[768,2048]{1,0:T(8,128)(2,1)S(1)}, bf16[768,2048]{1,0:T(8,128)(2,1)S(1)}) fusion(bf16[768,2048]{1,0:T(8,128)(2,1)} %collective-permute-done.7, f32[2048]{0:T(1024)S(1)} %get-tuple-element.23, f32[768]{0:T(1024)S(1)} %mul.72, f32[2048]{0:T(1024)S(1)} %get-tuple-element.24, bf16[768,2048]{1,0:T(8,128)(2,1)S(1)} %copy-done.5), kind=kLoop, calls=%fused_computation | loop fusion | flops 12582912 | bytes 12602368 | tf_op jit(solution)/shard_map/convert_element_type | solution.py:146
  181.0 0.8 broadcast_in_dim.30
  181.8 0.2 fusion.5
  182.1 0.2 fusion.4
  182.3 0.2 fusion.3
  182.5 0.2 fusion.2
  182.8 14.4 %collective-permute-done.8 = bf16[1024,256]{1,0:T(8,128)(2,1)S(1)} collective-permute-done((bf16[1024,256]{1,0:T(8,128)(2,1)}, bf16[1024,256]{1,0:T(8,128)(2,1)S(1)}, u32[]{:S(2)}, u32[]{:S(2)}) %collective-permute-start.8) | collective-permute-done | bytes 524320 | tf_op jit(solution)/shard_map/ppermute | solution.py:22
  197.2 0.6 fusion.16
  197.8 2.7 collective-permute-done.9
  200.5 0.6 fusion.12
  201.0 0.0 collective-permute-done.10
  201.1 0.6 fusion.8
  201.6 2.4 fusion.51
  204.0 0.9 collective-permute-start.11
  204.9 11.6 %all-to-all-start.4 = ((bf16[16,48,256]{2,1,0:T(8,128)(2,1)}), bf16[16,48,256]{2,1,0:T(8,128)(2,1)S(1)}, u32[]{:S(2)}, u32[]{:S(2)}) async-start(bf16[16,48,256]{2,1,0:T(8,128)(2,1)} %bitcast.21), calls=%async_computation.4 | async-start | bytes 786432 | tf_op jit(solution)/shard_map/all_to_all | solution.py:165
  216.6 1.3 collective-permute-start.12
  217.8 0.3 collective-permute-start.13
  218.1 0.0 collective-permute-done.11
  218.1 2.0 fusion.14
  220.1 0.0 copy-start.1
  220.1 18.5 %collective-permute-done.12 = bf16[1024,256]{1,0:T(8,128)(2,1)S(1)} collective-permute-done((bf16[1024,256]{1,0:T(8,128)(2,1)}, bf16[1024,256]{1,0:T(8,128)(2,1)S(1)}, u32[]{:S(2)}, u32[]{:S(2)}) %collective-permute-start.12) | collective-permute-done | bytes 524320 | tf_op jit(solution)/shard_map/ppermute | solution.py:22
  238.6 2.0 fusion.10
  240.6 0.0 collective-permute-done.13
  240.6 2.0 fusion.6
  242.6 2.9 %fusion.48 = bf16[768,256]{1,0:T(8,128)(2,1)} fusion(f32[768,256]{1,0:T(8,128)S(1)} %fusion.6, f32[768,256]{1,0:T(8,128)S(1)} %fusion.10, f32[768,256]{1,0:T(8,128)S(1)} %fusion.14, bf16[1024,256]{1,0:T(8,128)(2,1)} %bitcast.15, bf16[4,768,1024]{2,1,0:T(8,128)(2,1)} %copy-done.4, s32[]{:T(128)S(6)} %select_n.54), kind=kOutput, calls=%fused_computation.43 | convolution fusion | flops 403439616 | bytes 4849668 | tf_op jit(solution)/shard_map/dot_general | solution.py:36
  245.5 0.0 all-to-all-done.4.up_ref
  245.5 11.6 %all-to-all-start.3 = ((bf16[16,48,256]{2,1,0:T(8,128)(2,1)}), bf16[16,48,256]{2,1,0:T(8,128)(2,1)S(1)}, u32[]{:S(2)}, u32[]{:S(2)}) async-start(bf16[16,48,256]{2,1,0:T(8,128)(2,1)} %bitcast.20), calls=%async_computation.3 | async-start | bytes 786432 | tf_op jit(solution)/shard_map/all_to_all | solution.py:165
  257.1 1.0 shard_map.103.refs_0_
  258.2 15.9 %all-to-all-done.3.up_ref = bf16[16,48,256]{2,1,0:T(8,128)(2,1)S(1)} async-done(((bf16[16,48,256]{2,1,0:T(8,128)(2,1)}), bf16[16,48,256]{2,1,0:T(8,128)(2,1)S(1)}, u32[]{:S(2)}, u32[]{:S(2)}) %all-to-all-start.3) | async-done | bytes 393248 | tf_op jit(solution)/shard_map/all_to_all | solution.py:165
  274.1 1.0 shard_map.104
  (26 shorter events, 0.1 us)
Async XLA Ops:
  7.2 132.8 %copy-start.6 = (bf16[4096]{0:T(1024)(128)(2,1)S(1)}, bf16[4096]{0:T(1024)(128)(2,1)}, u32[]{:S(2)}) copy-start(bf16[4096]{0:T(1024)(128)(2,1)} %param.12) | copy-start | bytes 24580
  7.2 89.7 %all-gather.2.cloned.1.call-start = ((), (), s32[]{:S(2)}) async-start(), calls=%async_computation.5 | async-start | bytes 3342336 | tf_op jit(solution)/shard_map/all_gather | solution.py:122
  10.7 86.9 %collective-permute-start = (f32[16,128]{1,0:T(8,128)S(1)}, f32[16,128]{1,0:T(8,128)S(1)}, u32[]{:S(2)}, u32[]{:S(2)}) collective-permute-start(f32[16,128]{1,0:T(8,128)S(1)} %get-tuple-element.20), channel_id=1, source_target_pairs={{0,32},{32,64},{64,96},{96,0},{1,33},{33,65},{65,97},{97,1},{2,34}... | collective-permute-start | bytes 24584 | tf_op jit(solution)/shard_map/ppermute | solution.py:22
  10.9 86.7 %collective-permute-start.1 = (f32[16,128]{1,0:T(8,128)S(1)}, f32[16,128]{1,0:T(8,128)S(1)}, u32[]{:S(2)}, u32[]{:S(2)}) collective-permute-start(f32[16,128]{1,0:T(8,128)S(1)} %get-tuple-element.22), channel_id=1, source_target_pairs={{0,96},{32,0},{64,32},{96,64},{1,97},{33,1},{65,33},{97,65},{2,98}... | collective-permute-start | bytes 24584 | tf_op jit(solution)/shard_map/ppermute | solution.py:22
  12.9 84.8 %collective-permute-start.2 = (f32[16,128]{1,0:T(8,128)S(1)}, f32[16,128]{1,0:T(8,128)S(1)}, u32[]{:S(2)}, u32[]{:S(2)}) collective-permute-start(f32[16,128]{1,0:T(8,128)S(1)} %get-tuple-element.21), channel_id=1, source_target_pairs={{0,64},{32,96},{64,0},{96,32},{1,65},{33,97},{65,1},{97,33},{2,66}... | collective-permute-start | bytes 24584 | tf_op jit(solution)/shard_map/ppermute | solution.py:22
  14.0 1.2 collective-permute-start.3
  16.5 164.6 %copy-start.7 = (f32[64]{0:T(128)}, f32[64]{0:T(128)S(1)}, u32[]{:S(2)}) copy-start(f32[64]{0:T(128)S(1)} %get-tuple-element.19) | copy-start | bytes 772
  96.9 80.5 %collective-permute-start.7 = (bf16[768,2048]{1,0:T(8,128)(2,1)}, bf16[768,2048]{1,0:T(8,128)(2,1)}, u32[]{:S(2)}, u32[]{:S(2)}) collective-permute-start(bf16[768,2048]{1,0:T(8,128)(2,1)} %all-gather.2.cloned.1.call-done), channel_id=1, source_target_pairs={{0,1},{1,0},{2,3},{3,2},{4,5},{5,4},{6,7},{7,6},{8,9},{9,8},{10,11... | collective-permute-start | bytes 9437192 | tf_op jit(solution)/shard_map/ppermute | solution.py:123
  121.2 3.8 %collective-permute-start.4 = (f32[24,128]{1,0:T(8,128)S(1)}, f32[24,128]{1,0:T(8,128)S(1)}, u32[]{:S(2)}, u32[]{:S(2)}) collective-permute-start(f32[24,128]{1,0:T(8,128)S(1)} %reduce_sum.49.refs_0_), channel_id=1, source_target_pairs={{0,32},{32,64},{64,96},{96,0},{1,33},{33,65},{65,97},{97,1},{2,34}... | collective-permute-start | bytes 36872 | tf_op jit(solution)/shard_map/ppermute | solution.py:22
  121.9 4.9 %collective-permute-start.5 = (f32[24,128]{1,0:T(8,128)S(1)}, f32[24,128]{1,0:T(8,128)S(1)}, u32[]{:S(2)}, u32[]{:S(2)}) collective-permute-start(f32[24,128]{1,0:T(8,128)S(1)} %reduce_sum.49.refs_0_), channel_id=1, source_target_pairs={{0,96},{32,0},{64,32},{96,64},{1,97},{33,1},{65,33},{97,65},{2,98}... | collective-permute-start | bytes 36872 | tf_op jit(solution)/shard_map/ppermute | solution.py:22
  123.4 5.2 %collective-permute-start.6 = (f32[24,128]{1,0:T(8,128)S(1)}, f32[24,128]{1,0:T(8,128)S(1)}, u32[]{:S(2)}, u32[]{:S(2)}) collective-permute-start(f32[24,128]{1,0:T(8,128)S(1)} %reduce_sum.49.refs_0_), channel_id=1, source_target_pairs={{0,64},{32,96},{64,0},{96,32},{1,65},{33,97},{65,1},{97,33},{2,66}... | collective-permute-start | bytes 36872 | tf_op jit(solution)/shard_map/ppermute | solution.py:22
  128.6 1.2 copy-start
  129.8 1.2 copy-start.2
  131.0 0.8 copy-start.3
  131.8 45.6 %copy-start.5 = (bf16[768,2048]{1,0:T(8,128)(2,1)S(1)}, bf16[768,2048]{1,0:T(8,128)(2,1)}, u32[]{:S(2)}) copy-start(bf16[768,2048]{1,0:T(8,128)(2,1)} %all-gather.2.cloned.1.call-done) | copy-start | bytes 9437188
  133.5 33.1 %all-to-all-start.2 = ((bf16[16,64,256]{2,1,0:T(8,128)(2,1)}), bf16[16,64,256]{2,1,0:T(8,128)(2,1)}, u32[]{:S(2)}, u32[]{:S(2)}) async-start(bf16[16,64,256]{2,1,0:T(8,128)(2,1)} %get-tuple-element.13), calls=%async_computation.2 | async-start | bytes 1048576 | tf_op jit(solution)/shard_map/all_to_all | solution.py:154
  166.6 37.5 %all-to-all-start.1 = ((bf16[16,64,256]{2,1,0:T(8,128)(2,1)}), bf16[16,64,256]{2,1,0:T(8,128)(2,1)}, u32[]{:S(2)}, u32[]{:S(2)}) async-start(bf16[16,64,256]{2,1,0:T(8,128)(2,1)} %get-tuple-element.12), calls=%async_computation.1 | async-start | bytes 1048576 | tf_op jit(solution)/shard_map/all_to_all | solution.py:154
  173.8 23.4 %collective-permute-start.8 = (bf16[1024,256]{1,0:T(8,128)(2,1)}, bf16[1024,256]{1,0:T(8,128)(2,1)S(1)}, u32[]{:S(2)}, u32[]{:S(2)}) collective-permute-start(bf16[1024,256]{1,0:T(8,128)(2,1)} %bitcast.16), channel_id=1, source_target_pairs={{0,32},{32,64},{64,96},{96,0},{1,33},{33,65},{65,97},{97,1},{2,34}... | collective-permute-start | bytes 1572872 | tf_op jit(solution)/shard_map/ppermute | solution.py:22
  175.7 24.8 %collective-permute-start.9 = (bf16[1024,256]{1,0:T(8,128)(2,1)}, bf16[1024,256]{1,0:T(8,128)(2,1)S(1)}, u32[]{:S(2)}, u32[]{:S(2)}) collective-permute-start(bf16[1024,256]{1,0:T(8,128)(2,1)} %bitcast.16), channel_id=1, source_target_pairs={{0,96},{32,0},{64,32},{96,64},{1,97},{33,1},{65,33},{97,65},{2,98}... | collective-permute-start | bytes 1572872 | tf_op jit(solution)/shard_map/ppermute | solution.py:22
  176.0 25.1 %collective-permute-start.10 = (bf16[1024,256]{1,0:T(8,128)(2,1)}, bf16[1024,256]{1,0:T(8,128)(2,1)S(1)}, u32[]{:S(2)}, u32[]{:S(2)}) collective-permute-start(bf16[1024,256]{1,0:T(8,128)(2,1)} %bitcast.16), channel_id=1, source_target_pairs={{0,64},{32,96},{64,0},{96,32},{1,65},{33,97},{65,1},{97,33},{2,66}... | collective-permute-start | bytes 1572872 | tf_op jit(solution)/shard_map/ppermute | solution.py:22
  182.7 18.9 %copy-start.4 = (bf16[4,768,1024]{2,1,0:T(8,128)(2,1)}, bf16[4,768,1024]{2,1,0:T(8,128)(2,1)S(1)}, u32[]{:S(2)}) copy-start(bf16[4,768,1024]{2,1,0:T(8,128)(2,1)S(1)} %fusion.2) | copy-start | bytes 18874372
  204.0 14.1 %collective-permute-start.11 = (bf16[1024,256]{1,0:T(8,128)(2,1)}, bf16[1024,256]{1,0:T(8,128)(2,1)S(1)}, u32[]{:S(2)}, u32[]{:S(2)}) collective-permute-start(bf16[1024,256]{1,0:T(8,128)(2,1)} %bitcast.15), channel_id=1, source_target_pairs={{0,32},{32,64},{64,96},{96,0},{1,33},{33,65},{65,97},{97,1},{2,34}... | collective-permute-start | bytes 1572872 | tf_op jit(solution)/shard_map/ppermute | solution.py:22
  204.9 40.6 %all-to-all-start.4 = ((bf16[16,48,256]{2,1,0:T(8,128)(2,1)}), bf16[16,48,256]{2,1,0:T(8,128)(2,1)S(1)}, u32[]{:S(2)}, u32[]{:S(2)}) async-start(bf16[16,48,256]{2,1,0:T(8,128)(2,1)} %bitcast.21), calls=%async_computation.4 | async-start | bytes 786432 | tf_op jit(solution)/shard_map/all_to_all | solution.py:165
  216.6 22.1 %collective-permute-start.12 = (bf16[1024,256]{1,0:T(8,128)(2,1)}, bf16[1024,256]{1,0:T(8,128)(2,1)S(1)}, u32[]{:S(2)}, u32[]{:S(2)}) collective-permute-start(bf16[1024,256]{1,0:T(8,128)(2,1)} %bitcast.15), channel_id=1, source_target_pairs={{0,96},{32,0},{64,32},{96,64},{1,97},{33,1},{65,33},{97,65},{2,98}... | collective-permute-start | bytes 1572872 | tf_op jit(solution)/shard_map/ppermute | solution.py:22
  217.8 22.8 %collective-permute-start.13 = (bf16[1024,256]{1,0:T(8,128)(2,1)}, bf16[1024,256]{1,0:T(8,128)(2,1)S(1)}, u32[]{:S(2)}, u32[]{:S(2)}) collective-permute-start(bf16[1024,256]{1,0:T(8,128)(2,1)} %bitcast.15), channel_id=1, source_target_pairs={{0,64},{32,96},{64,0},{96,32},{1,65},{33,97},{65,1},{97,33},{2,66}... | collective-permute-start | bytes 1572872 | tf_op jit(solution)/shard_map/ppermute | solution.py:22
  220.1 37.0 %copy-start.1 = (bf16[48,8192]{1,0:T(8,128)(2,1)S(1)}, bf16[48,8192]{1,0:T(8,128)(2,1)}, u32[]{:S(2)}) copy-start(bf16[48,8192]{1,0:T(8,128)(2,1)} %gate_ref.3) | copy-start | bytes 2359300
  245.5 28.6 %all-to-all-start.3 = ((bf16[16,48,256]{2,1,0:T(8,128)(2,1)}), bf16[16,48,256]{2,1,0:T(8,128)(2,1)S(1)}, u32[]{:S(2)}, u32[]{:S(2)}) async-start(bf16[16,48,256]{2,1,0:T(8,128)(2,1)} %bitcast.20), calls=%async_computation.3 | async-start | bytes 786432 | tf_op jit(solution)/shard_map/all_to_all | solution.py:165
Sparse Core Ops, SparseCore 0:
  10.4 86.4 all-gather.1

commit v3 on v2

--- a/solution.py
+++ b/solution.py
@@ -11,6 +11,7 @@
 CHUNKS = 2
 LANES = 128
 VMEM_LIMIT = 16 * 2**20
+UPDATE_VMEM_LIMIT = 60500 * 2**10
 
 
 def steps(size):
@@ -32,10 +33,6 @@
     return total
 
 
-def dot(a, b):
-    return jnp.dot(a, b, preferred_element_type=jnp.float32)
-
-
 def vmem(n):
     return [pl.BlockSpec(memory_space=pltpu.VMEM)] * n
 
@@ -45,21 +42,36 @@
     share = col_moment.shape[0] // size
     width = local_columns // CHUNKS // n_z
 
+    half = local_columns // 2
+
     def kernel(me_ref, *refs):
         piece_refs, refs = refs[:size], refs[size:]
-        moment_ref, rows_ref, grad_ref, weight_ref, out_ref, columns_ref, *send_refs, factor_ref = refs
+        rows_ref, moment_hbm, grad_hbm, weight_hbm, out_ref, columns_ref, *send_refs = refs[: 6 + CHUNKS]
+        factor_ref, moment_ref, grad_ref, weight_ref, moment_sem, sems = refs[6 + CHUNKS :]
+        moment_copy = pltpu.make_async_copy(moment_hbm, moment_ref, moment_sem)
+        moment_copy.start()
+        copies = []
+        for i in range(2):
+            part = pl.ds(i * half, half)
+            for j, (source, target) in enumerate(((grad_hbm, grad_ref), (weight_hbm, weight_ref))):
+                copies.append(pltpu.make_async_copy(source.at[:, part], target.at[:, part], sems.at[i, j]))
+                copies[-1].start()
         rows_summed = 0.0
         for step, piece_ref in zip(steps(size), piece_refs, strict=True):
             source = lax.rem(me_ref[0] - step + size, size)
             place = pl.ds(pl.multiple_of(source * share, share), share)
             factor_ref[place, :] = piece_ref[:share, :]
             rows_summed += piece_ref[share : share + 1, LANES - 1 :]
+        moment_copy.wait()
         new_columns = 0.8 * moment_ref[...] + 0.2 * (factor_ref[...] / rows)
         columns_ref[...] = new_columns
         factor_ref[...] = 0.01 * jnp.sqrt((rows_summed / rows) / new_columns)
         row_factor = jnp.broadcast_to(1.0 / jnp.sqrt(rows_ref[...]), (local_rows, LANES))
         for group in range(local_columns // LANES):
             at = group * LANES
+            if at % half == 0:
+                for copy in copies[2 * (at // half) : 2 * (at // half) + 2]:
+                    copy.wait()
             part = slice(at, at + LANES)
             scaled = grad_ref[:, part].astype(jnp.float32) * row_factor * factor_ref[group : group + 1, :]
             new = (weight_ref[:, part].astype(jnp.float32) - scaled).astype(jnp.bfloat16)
@@ -76,11 +88,35 @@
             jax.ShapeDtypeStruct(col_moment.shape, jnp.float32),
             *[send] * CHUNKS,
         ],
-        in_specs=[pl.BlockSpec(memory_space=pltpu.SMEM), *vmem(size + 4)],
+        in_specs=[
+            pl.BlockSpec(memory_space=pltpu.SMEM),
+            *vmem(size + 1),
+            *[pl.BlockSpec(memory_space=pltpu.HBM)] * 3,
+        ],
         out_specs=vmem(2 + CHUNKS),
-        scratch_shapes=[pltpu.VMEM(col_moment.shape, jnp.float32)],
-        compiler_params=pltpu.CompilerParams(vmem_limit_bytes=VMEM_LIMIT),
-    )(me.reshape(1), *pieces, col_moment, new_rows.reshape(-1, 1), grad, weight)
+        scratch_shapes=[
+            pltpu.VMEM(col_moment.shape, jnp.float32),
+            pltpu.VMEM(col_moment.shape, jnp.float32),
+            pltpu.VMEM(grad.shape, grad.dtype),
+            pltpu.VMEM(weight.shape, weight.dtype),
+            pltpu.SemaphoreType.DMA,
+            pltpu.SemaphoreType.DMA((2, 2)),
+        ],
+        cost_estimate=pl.CostEstimate(flops=6 * grad.size, bytes_accessed=8 * grad.size, transcendentals=0),
+        compiler_params=pltpu.CompilerParams(vmem_limit_bytes=UPDATE_VMEM_LIMIT),
+    )(me.reshape(1), *pieces, new_rows.reshape(-1, 1), col_moment, grad, weight)
+
+
+def gather(x, axis):
+    size, me = lax.axis_size(axis), lax.axis_index(axis)
+    out = jnp.zeros((size, *x.shape), x.dtype)
+    for k in steps(size):
+        out = lax.dynamic_update_index_in_dim(out, shifted(x, axis, k), lax.rem(me - k + size, size), 0)
+    return out
+
+
+def dot(a, b):
+    return jnp.dot(a, b, preferred_element_type=jnp.float32)
 
 
 def finish(up, gate, hidden, chunk):
@@ -113,40 +149,43 @@
     local_rows, local_columns = grad.shape
     columns = local_columns * n_tp
     rows = local_rows * n_x * n_z
-    values = states.astype(jnp.float32)
-    scale = lax.rsqrt(jnp.mean(values * values, axis=1) + 1e-06)
-
-    features = states.shape[1]
-    share, piece = features // n_tp, features // n_x
-    tokens = lax.dynamic_slice_in_dim(states, me_tp * share, share, 1)
-    tokens = lax.all_gather(tokens, Z, axis=0, tiled=True)
-    other_tokens = lax.ppermute(tokens, "tp", [(0, 1), (1, 0)])
-
     gradient = grad.astype(jnp.float32)
     squares = gradient * gradient + 1e-30
     row_partial = jnp.sum(squares, axis=1)
     col_partial = jnp.sum(squares, axis=0).reshape(-1, LANES)
+    features = states.shape[1]
+    share = features // n_tp
+    tokens = lax.dynamic_slice_in_dim(states, me_tp * share, share, 1)
+    tokens = lax.all_gather(tokens, Z, axis=0, tiled=True)
+    other_tokens = lax.ppermute(tokens, "tp", [(0, 1), (1, 0)])
+    features = states.shape[1]
+    share = features // n_tp
+    tokens = lax.dynamic_slice_in_dim(states, me_tp * share, share, 1)
+    tokens = lax.all_gather(tokens, Z, axis=0, tiled=True)
+    other_tokens = lax.ppermute(tokens, "tp", [(0, 1), (1, 0)])
+    values = states.astype(jnp.float32)
+    scale = lax.rsqrt(jnp.mean(values * values, axis=1) + 1e-06)
     row_total = row_partial + lax.ppermute(row_partial, "tp", [(0, 1), (1, 0)])
     new_rows = 0.8 * row_moment + 0.2 * (row_total / columns)
     quarter = scatter_sum(col_partial, X)
-    n_quarter = quarter.shape[0]
-    extra = jnp.concatenate([scale, jnp.zeros((LANES - 1 - scale.shape[0],), jnp.float32), jnp.sum(new_rows).reshape(1)])
-    mine = jnp.concatenate([quarter, jnp.broadcast_to(extra, (8, LANES))])
+    n_quarter = quarter.size
+    tail = jnp.zeros((LANES,), jnp.float32).at[-1].set(jnp.sum(new_rows))
+    mine = jnp.concatenate([quarter.reshape(-1), tail])
     theirs = lax.all_to_all(jnp.broadcast_to(mine, (n_z, *mine.shape)), Z, 0, 0)
-    scales = theirs[:, n_quarter, : scale.shape[0]].reshape(-1, 1)
     mine = theirs.sum(axis=0)
+    tail = jnp.broadcast_to(mine[n_quarter:], (8, LANES))
+    mine = jnp.concatenate([mine[:n_quarter].reshape(-1, LANES), tail])
     pieces = [shifted(mine, X, k) for k in steps(n_x)]
     new_weight, new_columns, *sends = apply_update(
         pieces, me_x, col_moment.reshape(-1, LANES), new_rows, grad, weight, n_z, rows
     )
 
-    normed = jnp.zeros((n_x, tokens.shape[0], piece), jnp.bfloat16)
+    mean = sum(jnp.sum(jnp.square(t.astype(jnp.float32)), axis=1, keepdims=True) for t in (tokens, other_tokens)) / features
+    scales = lax.rsqrt(mean + 1e-06)
+    normed = []
     for part, half in ((tokens, me_tp), (other_tokens, n_tp - 1 - me_tp)):
         gain = lax.dynamic_slice_in_dim(norm_gain, half * share, share, 0).astype(jnp.float32)
-        part = (part.astype(jnp.float32) * scales * gain).astype(jnp.bfloat16)
-        for i in range(share // piece):
-            block = part[:, i * piece : (i + 1) * piece]
-            normed = lax.dynamic_update_index_in_dim(normed, block, half * (share // piece) + i, 0)
+        normed.append((part.astype(jnp.float32) * scales * gain).astype(jnp.bfloat16))
     normed = lax.optimization_barrier(normed)
 
     ups = []
@@ -154,15 +193,13 @@
         block = lax.all_to_all(send, Z, 0, 0).reshape(-1, send.shape[2])
         if ups:
             block, ups[-1] = lax.optimization_barrier((block, ups[-1]))
-        up = 0
-        for k in steps(n_x):
-            moved = shifted(block, X, k)
-            source = lax.rem(me_x - k + n_x, n_x)
-            up += dot(lax.dynamic_index_in_dim(normed, source, 0, keepdims=False), moved)
-        ups.append(up.astype(jnp.bfloat16))
+        block = gather(block, X).reshape(rows, -1)
+        up = dot(normed[0], lax.dynamic_slice_in_dim(block, me_tp * share, share, 0))
+        up += dot(normed[1], lax.dynamic_slice_in_dim(block, (n_tp - 1 - me_tp) * share, share, 0))
+        ups.append(up.astype(jnp.bfloat16).reshape(n_z, -1, up.shape[1]))
     hidden = None
     for c, up in enumerate(ups):
-        up = lax.all_to_all(up.reshape(n_z, -1, up.shape[1]), Z, 0, 0)
+        up = lax.all_to_all(up, Z, 0, 0)
         hidden = finish(up, gate_values, hidden, c)
     return (new_weight, new_rows, new_columns.reshape(-1), hidden)
 

time: 284 us -> 231 us (0.81)
  waiting for transfers between devices: 162 us -> 101 us
  blocking collectives: 23.5 us -> 39.5 us
  matrix products: 12.9 us -> 5.43 us
  starting transfers between devices: 49.9 us -> 43.5 us
  local copies, waits for them, and re-layouts: 6.75 us -> 10.6 us
    all_gather x1, waiting for transfers between devices: 80.4 us -> 42.8 us  [step(): tokens = lax.all_gather(tokens, Z, axis=0, tiled=True)]
    all_to_all x2, waiting for transfers between devices: 26.5 us -> 2.09 us  [step(): block = lax.all_to_all(send, Z, 0, 0).reshape(-1, send.shape[2])]
    all_to_all x1, blocking collectives: 23.5 us -> 39.5 us  [step(): theirs = lax.all_to_all(jnp.broadcast_to(mine, (n_z, *mine.shape)), Z, 0, 0)]
    all_to_all x2, waiting for transfers between devices: 15.9 us -> 28.3 us  [step(): up = lax.all_to_all(up, Z, 0, 0)]
    ppermute x12, waiting for transfers between devices: 39.3 us -> 27.6 us  [shifted(): lax.ppermute(x, axis, [(i, (i + step) % size) for i in range(size)])]
    all_to_all x2, starting transfers between devices: 23.3 us -> 13.3 us  [step(): up = lax.all_to_all(up, Z, 0, 0)]
    dot_general x8 -> x4, matrix products: 12.9 us -> 5.43 us  [dot(): return jnp.dot(a, b, preferred_element_type=jnp.float32)]
    ppermute x12, starting transfers between devices: 12.9 us -> 17.3 us  [shifted(): lax.ppermute(x, axis, [(i, (i + step) % size) for i in range(size)])]
  transfers between devices with their start and end apart: 19 -> 19, of which waited for: 9 -> 11; matrix products, arithmetic and copies ran while one was open for 8% -> 9% of each run, Pallas kernels for 1% -> 2%
where the time goes in v3:
time: 231 us; the launch traced here: 229 us
  waiting for transfers between devices  101 us (44%)
  starting transfers between devices  43.5 us (19%)
  blocking collectives  39.5 us (17%)
  between operations  14.4 us (6%)
  local copies, waits for them, and re-layouts  10.6 us (5%)
  other arithmetic  8.51 us (4%)
  Pallas kernels  5.82 us (3%)
  matrix products  5.43 us (2%)
    all_gather x1, waiting for transfers between devices, step(): tokens = lax.all_gather(tokens, Z, axis=0, tiled=True)  42.8 us
    all_to_all x1, blocking collectives, step(): theirs = lax.all_to_all(jnp.broadcast_to(mine, (n_z, *mine.shape)), Z, 0, 0)  39.5 us
    all_to_all x2, waiting for transfers between devices, step(): up = lax.all_to_all(up, Z, 0, 0)  28.3 us
    ppermute x12, waiting for transfers between devices, shifted(): lax.ppermute(x, axis, [(i, (i + step) % size) for i in range(size)])  27.6 us
    ppermute x12, starting transfers between devices, shifted(): lax.ppermute(x, axis, [(i, (i + step) % size) for i in range(size)])  17.3 us
    all_to_all x2, starting transfers between devices, step(): up = lax.all_to_all(up, Z, 0, 0)  13.3 us
    all_to_all x2, starting transfers between devices, step(): block = lax.all_to_all(send, Z, 0, 0).reshape(-1, send.shape[2])  12.7 us
    dot_general x4, matrix products, dot(): return jnp.dot(a, b, preferred_element_type=jnp.float32)  5.43 us
  transfers between devices with their start and end apart: 19, of which 11 were waited for; matrix products, arithmetic and copies ran while one was open for 9% of the time, Pallas kernels for 2%

profile of v3, /device:TPU:46, one launch (start us, length us, event | category | flops | bytes accessed | tf_op | source)
XLA Modules:
  0.0 228.6 jit_solution(17169631270277038349)
XLA Ops:
  7.2 0.0 copy-start
  7.2 0.1 all-gather.2.cloned.1.call-start
  7.3 0.9 copy-done
  8.2 0.7 constant_dynamic-slice_fusion
  8.9 0.1 all-gather.2.cloned.1.call-update
  8.9 1.7 fusion.7
  10.7 0.1 collective-permute-start.3
  10.8 1.3 collective-permute-start.2
  12.1 0.0 collective-permute-start.1
  12.1 3.2 %collective-permute-start = (f32[16,128]{1,0:T(8,128)S(1)}, f32[16,128]{1,0:T(8,128)S(1)}, u32[]{:S(2)}, u32[]{:S(2)}) collective-permute-start(f32[16,128]{1,0:T(8,128)S(1)} %get-tuple-element.36), channel_id=1, source_target_pairs={{0,32},{32,64},{64,96},{96,0},{1,33},{33,65},{65,97},{97,1},{2,34}... | collective-permute-start | bytes 24584 | tf_op jit(solution)/shard_map/ppermute | solution.py:23
  15.3 0.0 collective-permute-done.3
  15.3 1.3 fusion.23
  16.6 0.4 collective-permute-done.1
  17.0 0.7 select_maximum_fusion
  17.7 0.1 broadcast_in_dim.36
  17.8 39.5 %all_to_all.26 = f32[16,1,2176]{2,1,0:T(1,128)S(1)} all-to-all(f32[16,1,2176]{2,1,0:T(1,128)S(1)} %broadcast_in_dim.36), channel_id=1, replica_groups=mesh['job'=2,'fsdp_0'=4,'fsdp_1'=16,'tp'=2] {'fsdp_1'}, dimensions={0} | all-to-all | bytes 278528 | tf_op jit(solution)/shard_map/all_to_all | solution.py:174
  57.3 0.1 reduce_sum.57
  57.4 3.6 %collective-permute-start.4 = (f32[24,128]{1,0:T(8,128)S(1)}, f32[24,128]{1,0:T(8,128)S(1)}, u32[]{:S(2)}, u32[]{:S(2)}) collective-permute-start(f32[24,128]{1,0:T(8,128)S(1)} %pad_maximum_fusion.refs_0_), channel_id=1, source_target_pairs={{0,32},{32,64},{64,96},{96,0},{1,33},{33,65},{65,97},{97,1},{2,34}... | collective-permute-start | bytes 36872 | tf_op jit(solution)/shard_map/ppermute | solution.py:23
  61.0 1.6 collective-permute-start.6
  62.6 0.7 copy.15.refs_4_
  63.3 2.6 %collective-permute-done.5.refs_2_ = f32[24,128]{1,0:T(8,128)S(1)} collective-permute-done((f32[24,128]{1,0:T(8,128)S(1)}, f32[24,128]{1,0:T(8,128)S(1)}, u32[]{:S(2)}, u32[]{:S(2)}) %collective-permute-start.5) | collective-permute-done | bytes 12320 | tf_op jit(solution)/shard_map/ppermute | solution.py:23
  65.9 0.3 collective-permute-done.6.refs_3_
  66.2 0.3 copy-done.9
  66.5 0.3 copy-done.10
  66.8 3.8 %shard_map.102 = (bf16[64,8192]{1,0:T(8,128)(2,1)}, f32[64,128]{1,0:T(8,128)}, bf16[16,64,256]{2,1,0:T(8,128)(2,1)}, bf16[16,64,256]{2,1,0:T(8,128)(2,1)}) custom-call(s32[1]{0:T(128)} %bitcast.me_ref, f32[24,128]{1,0:T(8,128)} %copy-done.7, f32[24,128]{1,0:T(8,128)} %copy-done.8, f32[24,128]{1,0:T(8,128)} %copy-done.9, f32[24,128]{1,0:T(8,128)} %copy-done.10, ...), custom_call_target="tpu_custom_call" | custom-call | flops 3145728 | bytes 4194304 | tf_op jit(solution)/shard_map/pallas_call | solution.py:84
  70.7 4.6 %all-to-all-start.2 = ((bf16[16,64,256]{2,1,0:T(8,128)(2,1)}), bf16[16,64,256]{2,1,0:T(8,128)(2,1)}, u32[]{:S(2)}, u32[]{:S(2)}) async-start(bf16[16,64,256]{2,1,0:T(8,128)(2,1)} %get-tuple-element.28), calls=%async_computation.2 | async-start | bytes 1048576 | tf_op jit(solution)/shard_map/all_to_all | solution.py:193
  75.3 42.8 %all-gather.2.cloned.1.call-done = bf16[768,2048]{1,0:T(8,128)(2,1)} async-done(((bf16[48,2048]{1,0:T(8,128)(2,1)}), bf16[768,2048]{1,0:T(8,128)(2,1)}) %all-gather.2.cloned.1.call-update) | async-done | bytes 3145744 | tf_op jit(solution)/shard_map/all_gather | solution.py:164
  118.1 1.3 collective-permute-start.8
  119.4 0.7 collective-permute-start.9
  120.1 0.7 dynamic-slice_convert_fusion
  120.8 8.0 %all-to-all-start.1 = ((bf16[16,64,256]{2,1,0:T(8,128)(2,1)}), bf16[16,64,256]{2,1,0:T(8,128)(2,1)}, u32[]{:S(2)}, u32[]{:S(2)}) async-start(bf16[16,64,256]{2,1,0:T(8,128)(2,1)} %get-tuple-element.27), calls=%async_computation.1 | async-start | bytes 1048576 | tf_op jit(solution)/shard_map/all_to_all | solution.py:193
  128.9 1.9 collective-permute-start.10
  130.8 0.1 broadcast.44.clone
  130.9 1.2 bitcast_dynamic-update-slice_fusion.7
  132.2 0.6 collective-permute-done.8
  132.8 1.1 bitcast_dynamic-update-slice_fusion.6
  133.8 12.4 %collective-permute-done.9 = bf16[1024,256]{1,0:T(8,128)(2,1)} collective-permute-done((bf16[1024,256]{1,0:T(8,128)(2,1)}, bf16[1024,256]{1,0:T(8,128)(2,1)}, u32[]{:S(2)}, u32[]{:S(2)}) %collective-permute-start.9) | collective-permute-done | bytes 524320 | tf_op jit(solution)/shard_map/ppermute | solution.py:23
  146.2 1.1 bitcast_dynamic-update-slice_fusion.5
  147.3 0.0 collective-permute-done.10
  147.4 0.7 fusion
  148.1 0.0 collective-permute-done.7
  148.1 0.7 fusion.3
  148.8 2.6 %fusion.5 = (bf16[768,2048]{1,0:T(8,128)(2,1)S(1)}, bf16[768,2048]{1,0:T(8,128)(2,1)S(1)}) fusion(bf16[768,2048]{1,0:T(8,128)(2,1)S(1)} %collective-permute-done.7, f32[2048]{0:T(1024)S(1)} %get-tuple-element.39, f32[768]{0:T(1024)S(1)} %add_rsqrt_fusion, f32[2048]{0:T(1024)S(1)} %get-tuple-element.40, bf16[768,2048]{1,0:T(8,128)(2,1)S(1)} %copy-done.2), kind=kLoop, calls=%fused_computation.9 | loop fusion | flops 12582912 | bytes 12602368 | tf_op jit(solution)/shard_map/convert_element_type | solution.py:188
  151.4 1.6 copy-done.5
  153.0 1.0 fusion.13
  154.0 0.0 copy-done.3
  154.1 1.7 fusion.8
  155.8 2.1 all-to-all-done.1
  157.9 2.2 collective-permute-start.11
  160.1 1.5 collective-permute-start.13
  161.6 6.6 %all-to-all-start.4 = ((bf16[16,48,256]{2,1,0:T(8,128)(2,1)}), bf16[16,48,256]{2,1,0:T(8,128)(2,1)S(1)}, u32[]{:S(2)}, u32[]{:S(2)}) async-start(bf16[16,48,256]{2,1,0:T(8,128)(2,1)} %bitcast.19), calls=%async_computation.4 | async-start | bytes 786432 | tf_op jit(solution)/shard_map/all_to_all | solution.py:202
  168.2 0.1 broadcast.44
  168.3 1.2 bitcast_dynamic-update-slice_fusion.3
  169.6 3.3 %collective-permute-done.11 = bf16[1024,256]{1,0:T(8,128)(2,1)S(1)} collective-permute-done((bf16[1024,256]{1,0:T(8,128)(2,1)}, bf16[1024,256]{1,0:T(8,128)(2,1)S(1)}, u32[]{:S(2)}, u32[]{:S(2)}) %collective-permute-start.11) | collective-permute-done | bytes 524320 | tf_op jit(solution)/shard_map/ppermute | solution.py:23
  172.9 8.0 %collective-permute-done.12 = bf16[1024,256]{1,0:T(8,128)(2,1)S(1)} collective-permute-done((bf16[1024,256]{1,0:T(8,128)(2,1)}, bf16[1024,256]{1,0:T(8,128)(2,1)S(1)}, u32[]{:S(2)}, u32[]{:S(2)}) %collective-permute-start.12) | collective-permute-done | bytes 524320 | tf_op jit(solution)/shard_map/ppermute | solution.py:23
  181.0 0.0 collective-permute-done.13
  181.1 1.0 fusion.10
  182.1 0.9 copy-done.4
  183.0 1.7 fusion.9
  184.7 6.1 %all-to-all-done.4.up_ref = bf16[16,48,256]{2,1,0:T(8,128)(2,1)S(1)} async-done(((bf16[16,48,256]{2,1,0:T(8,128)(2,1)}), bf16[16,48,256]{2,1,0:T(8,128)(2,1)S(1)}, u32[]{:S(2)}, u32[]{:S(2)}) %all-to-all-start.4) | async-done | bytes 393248 | tf_op jit(solution)/shard_map/all_to_all | solution.py:202
  190.8 6.7 %all-to-all-start.3 = ((bf16[16,48,256]{2,1,0:T(8,128)(2,1)}), bf16[16,48,256]{2,1,0:T(8,128)(2,1)S(1)}, u32[]{:S(2)}, u32[]{:S(2)}) async-start(bf16[16,48,256]{2,1,0:T(8,128)(2,1)} %bitcast.25), calls=%async_computation.3 | async-start | bytes 786432 | tf_op jit(solution)/shard_map/all_to_all | solution.py:202
  197.6 1.0 shard_map.103.refs_0_
  198.6 22.2 %all-to-all-done.3.up_ref = bf16[16,48,256]{2,1,0:T(8,128)(2,1)S(1)} async-done(((bf16[16,48,256]{2,1,0:T(8,128)(2,1)}), bf16[16,48,256]{2,1,0:T(8,128)(2,1)S(1)}, u32[]{:S(2)}, u32[]{:S(2)}) %all-to-all-start.3) | async-done | bytes 393248 | tf_op jit(solution)/shard_map/all_to_all | solution.py:202
  220.7 1.0 shard_map.104
  (35 shorter events, 0.2 us)
Async XLA Ops:
  7.2 1.0 copy-start
  7.2 110.9 %all-gather.2.cloned.1.call-start = ((), (), s32[]{:S(2)}) async-start(), calls=%async_computation.5 | async-start | bytes 3342336 | tf_op jit(solution)/shard_map/all_gather | solution.py:164
  10.7 4.7 %collective-permute-start.3 = (f32[64]{0:T(128)S(1)}, f32[64]{0:T(128)S(1)}, u32[]{:S(2)}, u32[]{:S(2)}) collective-permute-start(f32[64]{0:T(128)S(1)} %get-tuple-element.33), channel_id=1, source_target_pairs={{0,1},{1,0},{2,3},{3,2},{4,5},{5,4},{6,7},{7,6},{8,9},{9,8},{10,11... | collective-permute-start | bytes 776 | tf_op jit(solution)/shard_map/ppermute | solution.py:168
  10.8 5.8 %collective-permute-start.2 = (f32[16,128]{1,0:T(8,128)S(1)}, f32[16,128]{1,0:T(8,128)S(1)}, u32[]{:S(2)}, u32[]{:S(2)}) collective-permute-start(f32[16,128]{1,0:T(8,128)S(1)} %get-tuple-element.37), channel_id=1, source_target_pairs={{0,64},{32,96},{64,0},{96,32},{1,65},{33,97},{65,1},{97,33},{2,66}... | collective-permute-start | bytes 24584 | tf_op jit(solution)/shard_map/ppermute | solution.py:23
  12.1 4.9 %collective-permute-start.1 = (f32[16,128]{1,0:T(8,128)S(1)}, f32[16,128]{1,0:T(8,128)S(1)}, u32[]{:S(2)}, u32[]{:S(2)}) collective-permute-start(f32[16,128]{1,0:T(8,128)S(1)} %get-tuple-element.38), channel_id=1, source_target_pairs={{0,96},{32,0},{64,32},{96,64},{1,97},{33,1},{65,33},{97,65},{2,98}... | collective-permute-start | bytes 24584 | tf_op jit(solution)/shard_map/ppermute | solution.py:23
  12.1 4.9 %collective-permute-start = (f32[16,128]{1,0:T(8,128)S(1)}, f32[16,128]{1,0:T(8,128)S(1)}, u32[]{:S(2)}, u32[]{:S(2)}) collective-permute-start(f32[16,128]{1,0:T(8,128)S(1)} %get-tuple-element.36), channel_id=1, source_target_pairs={{0,32},{32,64},{64,96},{96,0},{1,33},{33,65},{65,97},{97,1},{2,34}... | collective-permute-start | bytes 24584 | tf_op jit(solution)/shard_map/ppermute | solution.py:23
  16.6 58.7 %copy-start.11 = (f32[64]{0:T(128)}, f32[64]{0:T(128)S(1)}, u32[]{:S(2)}) copy-start(f32[64]{0:T(128)S(1)} %get-tuple-element.35) | copy-start | bytes 772
  57.4 8.8 %copy-start.7 = (f32[24,128]{1,0:T(8,128)}, f32[24,128]{1,0:T(8,128)S(1)}, u32[]{:S(2)}) copy-start(f32[24,128]{1,0:T(8,128)S(1)} %pad_maximum_fusion.refs_0_) | copy-start | bytes 36868
  57.4 5.9 %collective-permute-start.4 = (f32[24,128]{1,0:T(8,128)S(1)}, f32[24,128]{1,0:T(8,128)S(1)}, u32[]{:S(2)}, u32[]{:S(2)}) collective-permute-start(f32[24,128]{1,0:T(8,128)S(1)} %pad_maximum_fusion.refs_0_), channel_id=1, source_target_pairs={{0,32},{32,64},{64,96},{96,0},{1,33},{33,65},{65,97},{97,1},{2,34}... | collective-permute-start | bytes 36872 | tf_op jit(solution)/shard_map/ppermute | solution.py:23
  61.0 4.9 %collective-permute-start.5 = (f32[24,128]{1,0:T(8,128)S(1)}, f32[24,128]{1,0:T(8,128)S(1)}, u32[]{:S(2)}, u32[]{:S(2)}) collective-permute-start(f32[24,128]{1,0:T(8,128)S(1)} %pad_maximum_fusion.refs_0_), channel_id=1, source_target_pairs={{0,96},{32,0},{64,32},{96,64},{1,97},{33,1},{65,33},{97,65},{2,98}... | collective-permute-start | bytes 36872 | tf_op jit(solution)/shard_map/ppermute | solution.py:23
  61.0 5.2 %collective-permute-start.6 = (f32[24,128]{1,0:T(8,128)S(1)}, f32[24,128]{1,0:T(8,128)S(1)}, u32[]{:S(2)}, u32[]{:S(2)}) collective-permute-start(f32[24,128]{1,0:T(8,128)S(1)} %pad_maximum_fusion.refs_0_), channel_id=1, source_target_pairs={{0,64},{32,96},{64,0},{96,32},{1,65},{33,97},{65,1},{97,33},{2,66}... | collective-permute-start | bytes 36872 | tf_op jit(solution)/shard_map/ppermute | solution.py:23
  63.3 2.9 %copy-start.8 = (f32[24,128]{1,0:T(8,128)}, f32[24,128]{1,0:T(8,128)S(1)}, u32[]{:S(2)}) copy-start(f32[24,128]{1,0:T(8,128)S(1)} %collective-permute-done.4.refs_1_) | copy-start | bytes 36868
  65.9 0.6 copy-start.9
  66.2 0.6 copy-start.10
  70.7 47.5 %all-to-all-start.2 = ((bf16[16,64,256]{2,1,0:T(8,128)(2,1)}), bf16[16,64,256]{2,1,0:T(8,128)(2,1)}, u32[]{:S(2)}, u32[]{:S(2)}) async-start(bf16[16,64,256]{2,1,0:T(8,128)(2,1)} %get-tuple-element.28), calls=%async_computation.2 | async-start | bytes 1048576 | tf_op jit(solution)/shard_map/all_to_all | solution.py:193
  118.1 30.0 %collective-permute-start.7 = (bf16[768,2048]{1,0:T(8,128)(2,1)}, bf16[768,2048]{1,0:T(8,128)(2,1)S(1)}, u32[]{:S(2)}, u32[]{:S(2)}) collective-permute-start(bf16[768,2048]{1,0:T(8,128)(2,1)} %all-gather.2.cloned.1.call-done), channel_id=1, source_target_pairs={{0,1},{1,0},{2,3},{3,2},{4,5},{5,4},{6,7},{7,6},{8,9},{9,8},{10,11... | collective-permute-start | bytes 9437192 | tf_op jit(solution)/shard_map/ppermute | solution.py:165
  118.1 14.7 %collective-permute-start.8 = (bf16[1024,256]{1,0:T(8,128)(2,1)}, bf16[1024,256]{1,0:T(8,128)(2,1)}, u32[]{:S(2)}, u32[]{:S(2)}) collective-permute-start(bf16[1024,256]{1,0:T(8,128)(2,1)} %bitcast.14), channel_id=1, source_target_pairs={{0,32},{32,64},{64,96},{96,0},{1,33},{33,65},{65,97},{97,1},{2,34}... | collective-permute-start | bytes 1572872 | tf_op jit(solution)/shard_map/ppermute | solution.py:23
  119.4 26.8 %collective-permute-start.9 = (bf16[1024,256]{1,0:T(8,128)(2,1)}, bf16[1024,256]{1,0:T(8,128)(2,1)}, u32[]{:S(2)}, u32[]{:S(2)}) collective-permute-start(bf16[1024,256]{1,0:T(8,128)(2,1)} %bitcast.14), channel_id=1, source_target_pairs={{0,96},{32,0},{64,32},{96,64},{1,97},{33,1},{65,33},{97,65},{2,98}... | collective-permute-start | bytes 1572872 | tf_op jit(solution)/shard_map/ppermute | solution.py:23
  120.8 37.0 %all-to-all-start.1 = ((bf16[16,64,256]{2,1,0:T(8,128)(2,1)}), bf16[16,64,256]{2,1,0:T(8,128)(2,1)}, u32[]{:S(2)}, u32[]{:S(2)}) async-start(bf16[16,64,256]{2,1,0:T(8,128)(2,1)} %get-tuple-element.27), calls=%async_computation.1 | async-start | bytes 1048576 | tf_op jit(solution)/shard_map/all_to_all | solution.py:193
  128.9 18.4 %collective-permute-start.10 = (bf16[1024,256]{1,0:T(8,128)(2,1)}, bf16[1024,256]{1,0:T(8,128)(2,1)S(1)}, u32[]{:S(2)}, u32[]{:S(2)}) collective-permute-start(bf16[1024,256]{1,0:T(8,128)(2,1)} %bitcast.14), channel_id=1, source_target_pairs={{0,64},{32,96},{64,0},{96,32},{1,65},{33,97},{65,1},{97,33},{2,66}... | collective-permute-start | bytes 1572872 | tf_op jit(solution)/shard_map/ppermute | solution.py:23
  130.9 16.5 %copy-start.2 = (bf16[768,2048]{1,0:T(8,128)(2,1)S(1)}, bf16[768,2048]{1,0:T(8,128)(2,1)}, u32[]{:S(2)}) copy-start(bf16[768,2048]{1,0:T(8,128)(2,1)} %all-gather.2.cloned.1.call-done) | copy-start | bytes 9437188
  151.4 1.6 copy-start.5
  151.4 2.6 %copy-start.3 = (bf16[768,2048]{1,0:T(8,128)(2,1)}, bf16[768,2048]{1,0:T(8,128)(2,1)S(1)}, u32[]{:S(2)}) copy-start(bf16[768,2048]{1,0:T(8,128)(2,1)S(1)} %get-tuple-element.26) | copy-start | bytes 9437188
  157.9 15.0 %collective-permute-start.11 = (bf16[1024,256]{1,0:T(8,128)(2,1)}, bf16[1024,256]{1,0:T(8,128)(2,1)S(1)}, u32[]{:S(2)}, u32[]{:S(2)}) collective-permute-start(bf16[1024,256]{1,0:T(8,128)(2,1)} %bitcast.12), channel_id=1, source_target_pairs={{0,32},{32,64},{64,96},{96,0},{1,33},{33,65},{65,97},{97,1},{2,34}... | collective-permute-start | bytes 1572872 | tf_op jit(solution)/shard_map/ppermute | solution.py:23
  160.1 20.9 %collective-permute-start.12 = (bf16[1024,256]{1,0:T(8,128)(2,1)}, bf16[1024,256]{1,0:T(8,128)(2,1)S(1)}, u32[]{:S(2)}, u32[]{:S(2)}) collective-permute-start(bf16[1024,256]{1,0:T(8,128)(2,1)} %bitcast.12), channel_id=1, source_target_pairs={{0,96},{32,0},{64,32},{96,64},{1,97},{33,1},{65,33},{97,65},{2,98}... | collective-permute-start | bytes 1572872 | tf_op jit(solution)/shard_map/ppermute | solution.py:23
  160.1 20.9 %collective-permute-start.13 = (bf16[1024,256]{1,0:T(8,128)(2,1)}, bf16[1024,256]{1,0:T(8,128)(2,1)S(1)}, u32[]{:S(2)}, u32[]{:S(2)}) collective-permute-start(bf16[1024,256]{1,0:T(8,128)(2,1)} %bitcast.12), channel_id=1, source_target_pairs={{0,64},{32,96},{64,0},{96,32},{1,65},{33,97},{65,1},{97,33},{2,66}... | collective-permute-start | bytes 1572872 | tf_op jit(solution)/shard_map/ppermute | solution.py:23
  161.6 29.3 %all-to-all-start.4 = ((bf16[16,48,256]{2,1,0:T(8,128)(2,1)}), bf16[16,48,256]{2,1,0:T(8,128)(2,1)S(1)}, u32[]{:S(2)}, u32[]{:S(2)}) async-start(bf16[16,48,256]{2,1,0:T(8,128)(2,1)} %bitcast.19), calls=%async_computation.4 | async-start | bytes 786432 | tf_op jit(solution)/shard_map/all_to_all | solution.py:202
  168.3 12.8 %copy-start.6 = (bf16[768,2048]{1,0:T(8,128)(2,1)S(1)}, bf16[768,2048]{1,0:T(8,128)(2,1)}, u32[]{:S(2)}) copy-start(bf16[768,2048]{1,0:T(8,128)(2,1)} %copy-done.5) | copy-start | bytes 9437188
  181.1 1.9 copy-start.4
  183.0 14.6 %copy-start.1 = (bf16[48,8192]{1,0:T(8,128)(2,1)S(1)}, bf16[48,8192]{1,0:T(8,128)(2,1)}, u32[]{:S(2)}) copy-start(bf16[48,8192]{1,0:T(8,128)(2,1)} %gate_ref.3) | copy-start | bytes 2359300
  190.8 29.9 %all-to-all-start.3 = ((bf16[16,48,256]{2,1,0:T(8,128)(2,1)}), bf16[16,48,256]{2,1,0:T(8,128)(2,1)S(1)}, u32[]{:S(2)}, u32[]{:S(2)}) async-start(bf16[16,48,256]{2,1,0:T(8,128)(2,1)} %bitcast.25), calls=%async_computation.3 | async-start | bytes 786432 | tf_op jit(solution)/shard_map/all_to_all | solution.py:202
Sparse Core Ops, SparseCore 0:
  9.8 108.2 all-gather.1

commit v4 on v3

--- a/solution.py
+++ b/solution.py
@@ -111,7 +111,8 @@
     size, me = lax.axis_size(axis), lax.axis_index(axis)
     out = jnp.zeros((size, *x.shape), x.dtype)
     for k in steps(size):
-        out = lax.dynamic_update_index_in_dim(out, shifted(x, axis, k), lax.rem(me - k + size, size), 0)
+        moved = shifted(x, axis, k)
+        out = lax.dynamic_update_index_in_dim(out, moved, lax.rem(me - k + size, size), 0)
     return out
 
 
@@ -169,9 +170,13 @@
     new_rows = 0.8 * row_moment + 0.2 * (row_total / columns)
     quarter = scatter_sum(col_partial, X)
     n_quarter = quarter.size
-    tail = jnp.zeros((LANES,), jnp.float32).at[-1].set(jnp.sum(new_rows))
+    values = states.astype(jnp.float32)
+    scale = lax.rsqrt(jnp.mean(values * values, axis=1) + 1e-06)
+    gap = jnp.zeros((LANES - 1 - scale.size,), jnp.float32)
+    tail = jnp.concatenate([scale, gap, jnp.sum(new_rows).reshape(1)])
     mine = jnp.concatenate([quarter.reshape(-1), tail])
     theirs = lax.all_to_all(jnp.broadcast_to(mine, (n_z, *mine.shape)), Z, 0, 0)
+    scales = theirs[:, n_quarter : n_quarter + scale.size].reshape(-1, 1)
     mine = theirs.sum(axis=0)
     tail = jnp.broadcast_to(mine[n_quarter:], (8, LANES))
     mine = jnp.concatenate([mine[:n_quarter].reshape(-1, LANES), tail])
@@ -180,8 +185,6 @@
         pieces, me_x, col_moment.reshape(-1, LANES), new_rows, grad, weight, n_z, rows
     )
 
-    mean = sum(jnp.sum(jnp.square(t.astype(jnp.float32)), axis=1, keepdims=True) for t in (tokens, other_tokens)) / features
-    scales = lax.rsqrt(mean + 1e-06)
     normed = []
     for part, half in ((tokens, me_tp), (other_tokens, n_tp - 1 - me_tp)):
         gain = lax.dynamic_slice_in_dim(norm_gain, half * share, share, 0).astype(jnp.float32)

time: 231 us -> 232 us (level)
  waiting for transfers between devices: 101 us -> 104 us
  starting transfers between devices: 43.5 us -> 40.6 us
  other arithmetic: 8.51 us -> 6.08 us
    ppermute x12, starting transfers between devices: 17.3 us -> 14.8 us  [shifted(): lax.ppermute(x, axis, [(i, (i + step) % size) for i in range(size)])]
  transfers between devices with their start and end apart: 19 -> 19, of which waited for: 11 -> 10; matrix products, arithmetic and copies ran while one was open for 9% -> 8% of each run, Pallas kernels for 2% -> 2%
where the time goes in v4:
time: 232 us; the launch traced here: 229 us
  waiting for transfers between devices  104 us (45%)
  blocking collectives  40.7 us (18%)
  starting transfers between devices  40.6 us (18%)
  between operations  14.4 us (6%)
  local copies, waits for them, and re-layouts  11.4 us (5%)
  other arithmetic  6.08 us (3%)
  Pallas kernels  5.83 us (3%)
  matrix products  5.45 us (2%)
    all_gather x1, waiting for transfers between devices, step(): tokens = lax.all_gather(tokens, Z, axis=0, tiled=True)  44.2 us
    all_to_all x1, blocking collectives, step(): theirs = lax.all_to_all(jnp.broadcast_to(mine, (n_z, *mine.shape)), Z, 0, 0)  40.7 us
    all_to_all x2, waiting for transfers between devices, step(): up = lax.all_to_all(up, Z, 0, 0)  28.6 us
    ppermute x12, waiting for transfers between devices, shifted(): lax.ppermute(x, axis, [(i, (i + step) % size) for i in range(size)])  27.4 us
    ppermute x12, starting transfers between devices, shifted(): lax.ppermute(x, axis, [(i, (i + step) % size) for i in range(size)])  14.8 us
    all_to_all x2, starting transfers between devices, step(): up = lax.all_to_all(up, Z, 0, 0)  13.3 us
    all_to_all x2, starting transfers between devices, step(): block = lax.all_to_all(send, Z, 0, 0).reshape(-1, send.shape[2])  12.5 us
    dot_general x4, matrix products, dot(): return jnp.dot(a, b, preferred_element_type=jnp.float32)  5.45 us
  transfers between devices with their start and end apart: 19, of which 10 were waited for; matrix products, arithmetic and copies ran while one was open for 8% of the time, Pallas kernels for 2%

profile of v4, /device:TPU:46, one launch (start us, length us, event | category | flops | bytes accessed | tf_op | source)
XLA Modules:
  0.0 228.6 jit_solution(14718569666934966231)
XLA Ops:
  7.2 0.1 all-gather.2.cloned.1.call-start
  7.3 1.6 constant_dynamic-slice_fusion
  8.9 0.1 all-gather.2.cloned.1.call-update
  9.0 1.7 fusion
  10.7 1.3 collective-permute-start.2
  12.0 3.2 %collective-permute-start = (f32[16,128]{1,0:T(8,128)S(1)}, f32[16,128]{1,0:T(8,128)S(1)}, u32[]{:S(2)}, u32[]{:S(2)}) collective-permute-start(f32[16,128]{1,0:T(8,128)S(1)} %get-tuple-element.24), channel_id=1, source_target_pairs={{0,32},{32,64},{64,96},{96,0},{1,33},{33,65},{65,97},{97,1},{2,34}... | collective-permute-start | bytes 24584 | tf_op jit(solution)/shard_map/ppermute | solution.py:23
  15.2 0.0 collective-permute-start.3
  15.2 1.2 multiply_reduce_fusion
  16.4 0.0 copy-start.10
  16.4 0.0 collective-permute-done.3
  16.4 0.6 fusion.17
  17.0 0.0 collective-permute-done
  17.1 0.7 concatenate.6
  17.8 0.1 broadcast_in_dim.37
  17.9 40.7 %all_to_all.29 = f32[16,1,2176]{2,1,0:T(1,128)S(1)} all-to-all(f32[16,1,2176]{2,1,0:T(1,128)S(1)} %broadcast_in_dim.37), channel_id=1, replica_groups=mesh['job'=2,'fsdp_0'=4,'fsdp_1'=16,'tp'=2] {'fsdp_1'}, dimensions={0} | all-to-all | bytes 278528 | tf_op jit(solution)/shard_map/all_to_all | solution.py:178
  58.6 0.1 reduce_sum.49
  58.7 2.0 collective-permute-start.4
  60.7 0.1 collective-permute-start.5
  60.8 1.6 collective-permute-start.6
  62.5 0.7 copy.15.refs_4_
  63.2 0.0 collective-permute-done.4.refs_1_
  63.2 2.4 %collective-permute-done.5.refs_2_ = f32[24,128]{1,0:T(8,128)S(1)} collective-permute-done((f32[24,128]{1,0:T(8,128)S(1)}, f32[24,128]{1,0:T(8,128)S(1)}, u32[]{:S(2)}, u32[]{:S(2)}) %collective-permute-start.5) | collective-permute-done | bytes 12320 | tf_op jit(solution)/shard_map/ppermute | solution.py:23
  65.6 0.4 collective-permute-done.6.refs_3_
  66.1 0.2 copy-done.8
  66.2 0.4 copy-done.9
  66.6 3.8 %shard_map.102 = (bf16[64,8192]{1,0:T(8,128)(2,1)}, f32[64,128]{1,0:T(8,128)}, bf16[16,64,256]{2,1,0:T(8,128)(2,1)}, bf16[16,64,256]{2,1,0:T(8,128)(2,1)}) custom-call(s32[1]{0:T(128)} %bitcast.me_ref, f32[24,128]{1,0:T(8,128)} %copy-done.6, f32[24,128]{1,0:T(8,128)} %copy-done.7, f32[24,128]{1,0:T(8,128)} %copy-done.8, f32[24,128]{1,0:T(8,128)} %copy-done.9, ...), custom_call_target="tpu_custom_call" | custom-call | flops 3145728 | bytes 4194304 | tf_op jit(solution)/shard_map/pallas_call | solution.py:84
  70.5 4.6 %all-to-all-start.2 = ((bf16[16,64,256]{2,1,0:T(8,128)(2,1)}), bf16[16,64,256]{2,1,0:T(8,128)(2,1)}, u32[]{:S(2)}, u32[]{:S(2)}) async-start(bf16[16,64,256]{2,1,0:T(8,128)(2,1)} %get-tuple-element.16), calls=%async_computation.2 | async-start | bytes 1048576 | tf_op jit(solution)/shard_map/all_to_all | solution.py:196
  75.1 44.2 %all-gather.2.cloned.1.call-done = bf16[768,2048]{1,0:T(8,128)(2,1)} async-done(((bf16[48,2048]{1,0:T(8,128)(2,1)}), bf16[768,2048]{1,0:T(8,128)(2,1)}) %all-gather.2.cloned.1.call-update) | async-done | bytes 3145744 | tf_op jit(solution)/shard_map/all_gather | solution.py:165
  119.4 0.0 collective-permute-start.7
  119.4 0.0 all-to-all-done.2
  119.4 0.2 collective-permute-start.8
  119.6 1.8 collective-permute-start.9
  121.4 0.1 mul.68
  121.5 7.8 %all-to-all-start.1 = ((bf16[16,64,256]{2,1,0:T(8,128)(2,1)}), bf16[16,64,256]{2,1,0:T(8,128)(2,1)}, u32[]{:S(2)}, u32[]{:S(2)}) async-start(bf16[16,64,256]{2,1,0:T(8,128)(2,1)} %get-tuple-element.15), calls=%async_computation.1 | async-start | bytes 1048576 | tf_op jit(solution)/shard_map/all_to_all | solution.py:196
  129.3 1.3 collective-permute-start.10
  130.6 0.1 broadcast.19.clone
  130.7 1.2 bitcast_dynamic-update-slice_fusion.7
  132.0 2.5 %collective-permute-done.8 = bf16[1024,256]{1,0:T(8,128)(2,1)} collective-permute-done((bf16[1024,256]{1,0:T(8,128)(2,1)}, bf16[1024,256]{1,0:T(8,128)(2,1)}, u32[]{:S(2)}, u32[]{:S(2)}) %collective-permute-start.8) | collective-permute-done | bytes 524320 | tf_op jit(solution)/shard_map/ppermute | solution.py:23
  134.5 1.1 bitcast_dynamic-update-slice_fusion.6
  135.6 10.9 %collective-permute-done.9 = bf16[1024,256]{1,0:T(8,128)(2,1)} collective-permute-done((bf16[1024,256]{1,0:T(8,128)(2,1)}, bf16[1024,256]{1,0:T(8,128)(2,1)}, u32[]{:S(2)}, u32[]{:S(2)}) %collective-permute-start.9) | collective-permute-done | bytes 524320 | tf_op jit(solution)/shard_map/ppermute | solution.py:23
  146.5 1.1 bitcast_dynamic-update-slice_fusion.5
  147.6 0.0 collective-permute-done.7
  147.6 2.5 %multiply_convert_fusion = (bf16[768,2048]{1,0:T(8,128)(2,1)S(1)}, bf16[768,2048]{1,0:T(8,128)(2,1)S(1)}) fusion(bf16[768,2048]{1,0:T(8,128)(2,1)S(1)} %collective-permute-done.7, f32[2048]{0:T(1024)S(1)} %get-tuple-element.27, f32[768]{0:T(1024)S(1)} %mul.68, f32[2048]{0:T(1024)S(1)} %get-tuple-element.28, bf16[768,2048]{1,0:T(8,128)(2,1)S(1)} %copy-done.1), kind=kLoop, calls=%fused_computation | loop fusion | flops 12582912 | bytes 12602368 | tf_op jit(solution)/shard_map/convert_element_type | solution.py:191
  150.1 1.6 copy-done.4
  151.7 1.0 fusion.7
  152.7 0.0 copy-done.2
  152.8 1.7 fusion.2
  154.5 3.9 %all-to-all-done.1 = bf16[16,64,256]{2,1,0:T(8,128)(2,1)} async-done(((bf16[16,64,256]{2,1,0:T(8,128)(2,1)}), bf16[16,64,256]{2,1,0:T(8,128)(2,1)}, u32[]{:S(2)}, u32[]{:S(2)}) %all-to-all-start.1) | async-done | bytes 524320 | tf_op jit(solution)/shard_map/all_to_all | solution.py:196
  158.4 1.8 collective-permute-start.11
  160.1 0.3 collective-permute-start.12
  160.4 1.2 collective-permute-start.13
  161.6 6.6 %all-to-all-start.4 = ((bf16[16,48,256]{2,1,0:T(8,128)(2,1)}), bf16[16,48,256]{2,1,0:T(8,128)(2,1)S(1)}, u32[]{:S(2)}, u32[]{:S(2)}) async-start(bf16[16,48,256]{2,1,0:T(8,128)(2,1)} %bitcast.19), calls=%async_computation.4 | async-start | bytes 786432 | tf_op jit(solution)/shard_map/all_to_all | solution.py:205
  168.2 0.1 broadcast.19
  168.4 1.2 bitcast_dynamic-update-slice_fusion.3
  169.6 7.8 %collective-permute-done.11 = bf16[1024,256]{1,0:T(8,128)(2,1)S(1)} collective-permute-done((bf16[1024,256]{1,0:T(8,128)(2,1)}, bf16[1024,256]{1,0:T(8,128)(2,1)S(1)}, u32[]{:S(2)}, u32[]{:S(2)}) %collective-permute-start.11) | collective-permute-done | bytes 524320 | tf_op jit(solution)/shard_map/ppermute | solution.py:23
  177.5 3.2 %collective-permute-done.12 = bf16[1024,256]{1,0:T(8,128)(2,1)S(1)} collective-permute-done((bf16[1024,256]{1,0:T(8,128)(2,1)}, bf16[1024,256]{1,0:T(8,128)(2,1)S(1)}, u32[]{:S(2)}, u32[]{:S(2)}) %collective-permute-start.12) | collective-permute-done | bytes 524320 | tf_op jit(solution)/shard_map/ppermute | solution.py:23
  180.8 1.0 fusion.4
  181.8 0.9 copy-done.3
  182.7 1.7 fusion.3
  184.5 6.4 %all-to-all-done.4.up_ref = bf16[16,48,256]{2,1,0:T(8,128)(2,1)S(1)} async-done(((bf16[16,48,256]{2,1,0:T(8,128)(2,1)}), bf16[16,48,256]{2,1,0:T(8,128)(2,1)S(1)}, u32[]{:S(2)}, u32[]{:S(2)}) %all-to-all-start.4) | async-done | bytes 393248 | tf_op jit(solution)/shard_map/all_to_all | solution.py:205
  190.8 6.7 %all-to-all-start.3 = ((bf16[16,48,256]{2,1,0:T(8,128)(2,1)}), bf16[16,48,256]{2,1,0:T(8,128)(2,1)S(1)}, u32[]{:S(2)}, u32[]{:S(2)}) async-start(bf16[16,48,256]{2,1,0:T(8,128)(2,1)} %bitcast.25), calls=%async_computation.3 | async-start | bytes 786432 | tf_op jit(solution)/shard_map/all_to_all | solution.py:205
  197.6 1.0 shard_map.103.refs_0_
  198.6 22.2 %all-to-all-done.3.up_ref = bf16[16,48,256]{2,1,0:T(8,128)(2,1)S(1)} async-done(((bf16[16,48,256]{2,1,0:T(8,128)(2,1)}), bf16[16,48,256]{2,1,0:T(8,128)(2,1)S(1)}, u32[]{:S(2)}, u32[]{:S(2)}) %all-to-all-start.3) | async-done | bytes 393248 | tf_op jit(solution)/shard_map/all_to_all | solution.py:205
  220.8 1.0 shard_map.104
  (40 shorter events, 0.3 us)
Async XLA Ops:
  7.2 9.2 %copy-start.12 = (f32[64]{0:T(128)S(1)}, f32[64]{0:T(128)}, u32[]{:S(2)}) copy-start(f32[64]{0:T(128)} %param.9) | copy-start | bytes 772
  7.2 112.2 %all-gather.2.cloned.1.call-start = ((), (), s32[]{:S(2)}) async-start(), calls=%async_computation.5 | async-start | bytes 3342336 | tf_op jit(solution)/shard_map/all_gather | solution.py:165
  10.7 6.3 %collective-permute-start.2 = (f32[16,128]{1,0:T(8,128)S(1)}, f32[16,128]{1,0:T(8,128)S(1)}, u32[]{:S(2)}, u32[]{:S(2)}) collective-permute-start(f32[16,128]{1,0:T(8,128)S(1)} %get-tuple-element.25), channel_id=1, source_target_pairs={{0,64},{32,96},{64,0},{96,32},{1,65},{33,97},{65,1},{97,33},{2,66}... | collective-permute-start | bytes 24584 | tf_op jit(solution)/shard_map/ppermute | solution.py:23
  12.0 5.1 %collective-permute-start.1 = (f32[16,128]{1,0:T(8,128)S(1)}, f32[16,128]{1,0:T(8,128)S(1)}, u32[]{:S(2)}, u32[]{:S(2)}) collective-permute-start(f32[16,128]{1,0:T(8,128)S(1)} %get-tuple-element.26), channel_id=1, source_target_pairs={{0,96},{32,0},{64,32},{96,64},{1,97},{33,1},{65,33},{97,65},{2,98}... | collective-permute-start | bytes 24584 | tf_op jit(solution)/shard_map/ppermute | solution.py:23
  12.0 5.1 %collective-permute-start = (f32[16,128]{1,0:T(8,128)S(1)}, f32[16,128]{1,0:T(8,128)S(1)}, u32[]{:S(2)}, u32[]{:S(2)}) collective-permute-start(f32[16,128]{1,0:T(8,128)S(1)} %get-tuple-element.24), channel_id=1, source_target_pairs={{0,32},{32,64},{64,96},{96,0},{1,33},{33,65},{65,97},{97,1},{2,34}... | collective-permute-start | bytes 24584 | tf_op jit(solution)/shard_map/ppermute | solution.py:23
  15.2 1.2 collective-permute-start.3
  16.4 105.0 %copy-start.10 = (bf16[4096]{0:T(1024)(128)(2,1)S(1)}, bf16[4096]{0:T(1024)(128)(2,1)}, u32[]{:S(2)}) copy-start(bf16[4096]{0:T(1024)(128)(2,1)} %param.12) | copy-start | bytes 24580
  17.0 104.4 %copy-start.11 = (f32[64]{0:T(128)}, f32[64]{0:T(128)S(1)}, u32[]{:S(2)}) copy-start(f32[64]{0:T(128)S(1)} %get-tuple-element.23) | copy-start | bytes 772
  58.7 7.4 %copy-start.6 = (f32[24,128]{1,0:T(8,128)}, f32[24,128]{1,0:T(8,128)S(1)}, u32[]{:S(2)}) copy-start(f32[24,128]{1,0:T(8,128)S(1)} %pad_maximum_fusion.refs_0_) | copy-start | bytes 36868
  58.7 4.5 %collective-permute-start.4 = (f32[24,128]{1,0:T(8,128)S(1)}, f32[24,128]{1,0:T(8,128)S(1)}, u32[]{:S(2)}, u32[]{:S(2)}) collective-permute-start(f32[24,128]{1,0:T(8,128)S(1)} %pad_maximum_fusion.refs_0_), channel_id=1, source_target_pairs={{0,32},{32,64},{64,96},{96,0},{1,33},{33,65},{65,97},{97,1},{2,34}... | collective-permute-start | bytes 36872 | tf_op jit(solution)/shard_map/ppermute | solution.py:23
  60.7 4.9 %collective-permute-start.5 = (f32[24,128]{1,0:T(8,128)S(1)}, f32[24,128]{1,0:T(8,128)S(1)}, u32[]{:S(2)}, u32[]{:S(2)}) collective-permute-start(f32[24,128]{1,0:T(8,128)S(1)} %pad_maximum_fusion.refs_0_), channel_id=1, source_target_pairs={{0,96},{32,0},{64,32},{96,64},{1,97},{33,1},{65,33},{97,65},{2,98}... | collective-permute-start | bytes 36872 | tf_op jit(solution)/shard_map/ppermute | solution.py:23
  60.8 5.2 %collective-permute-start.6 = (f32[24,128]{1,0:T(8,128)S(1)}, f32[24,128]{1,0:T(8,128)S(1)}, u32[]{:S(2)}, u32[]{:S(2)}) collective-permute-start(f32[24,128]{1,0:T(8,128)S(1)} %pad_maximum_fusion.refs_0_), channel_id=1, source_target_pairs={{0,64},{32,96},{64,0},{96,32},{1,65},{33,97},{65,1},{97,33},{2,66}... | collective-permute-start | bytes 36872 | tf_op jit(solution)/shard_map/ppermute | solution.py:23
  63.2 2.9 %copy-start.7 = (f32[24,128]{1,0:T(8,128)}, f32[24,128]{1,0:T(8,128)S(1)}, u32[]{:S(2)}) copy-start(f32[24,128]{1,0:T(8,128)S(1)} %collective-permute-done.4.refs_1_) | copy-start | bytes 36868
  65.6 0.6 copy-start.8
  66.0 0.6 copy-start.9
  70.5 48.9 %all-to-all-start.2 = ((bf16[16,64,256]{2,1,0:T(8,128)(2,1)}), bf16[16,64,256]{2,1,0:T(8,128)(2,1)}, u32[]{:S(2)}, u32[]{:S(2)}) async-start(bf16[16,64,256]{2,1,0:T(8,128)(2,1)} %get-tuple-element.16), calls=%async_computation.2 | async-start | bytes 1048576 | tf_op jit(solution)/shard_map/all_to_all | solution.py:196
  119.4 28.3 %collective-permute-start.7 = (bf16[768,2048]{1,0:T(8,128)(2,1)}, bf16[768,2048]{1,0:T(8,128)(2,1)S(1)}, u32[]{:S(2)}, u32[]{:S(2)}) collective-permute-start(bf16[768,2048]{1,0:T(8,128)(2,1)} %all-gather.2.cloned.1.call-done), channel_id=1, source_target_pairs={{0,1},{1,0},{2,3},{3,2},{4,5},{5,4},{6,7},{7,6},{8,9},{9,8},{10,11... | collective-permute-start | bytes 9437192 | tf_op jit(solution)/shard_map/ppermute | solution.py:166
  119.4 15.1 %collective-permute-start.8 = (bf16[1024,256]{1,0:T(8,128)(2,1)}, bf16[1024,256]{1,0:T(8,128)(2,1)}, u32[]{:S(2)}, u32[]{:S(2)}) collective-permute-start(bf16[1024,256]{1,0:T(8,128)(2,1)} %bitcast.14), channel_id=1, source_target_pairs={{0,32},{32,64},{64,96},{96,0},{1,33},{33,65},{65,97},{97,1},{2,34}... | collective-permute-start | bytes 1572872 | tf_op jit(solution)/shard_map/ppermute | solution.py:23
  119.6 26.9 %collective-permute-start.9 = (bf16[1024,256]{1,0:T(8,128)(2,1)}, bf16[1024,256]{1,0:T(8,128)(2,1)}, u32[]{:S(2)}, u32[]{:S(2)}) collective-permute-start(bf16[1024,256]{1,0:T(8,128)(2,1)} %bitcast.14), channel_id=1, source_target_pairs={{0,96},{32,0},{64,32},{96,64},{1,97},{33,1},{65,33},{97,65},{2,98}... | collective-permute-start | bytes 1572872 | tf_op jit(solution)/shard_map/ppermute | solution.py:23
  121.5 36.8 %all-to-all-start.1 = ((bf16[16,64,256]{2,1,0:T(8,128)(2,1)}), bf16[16,64,256]{2,1,0:T(8,128)(2,1)}, u32[]{:S(2)}, u32[]{:S(2)}) async-start(bf16[16,64,256]{2,1,0:T(8,128)(2,1)} %get-tuple-element.15), calls=%async_computation.1 | async-start | bytes 1048576 | tf_op jit(solution)/shard_map/all_to_all | solution.py:196
  129.3 18.2 %collective-permute-start.10 = (bf16[1024,256]{1,0:T(8,128)(2,1)}, bf16[1024,256]{1,0:T(8,128)(2,1)S(1)}, u32[]{:S(2)}, u32[]{:S(2)}) collective-permute-start(bf16[1024,256]{1,0:T(8,128)(2,1)} %bitcast.14), channel_id=1, source_target_pairs={{0,64},{32,96},{64,0},{96,32},{1,65},{33,97},{65,1},{97,33},{2,66}... | collective-permute-start | bytes 1572872 | tf_op jit(solution)/shard_map/ppermute | solution.py:23
  130.7 16.9 %copy-start.1 = (bf16[768,2048]{1,0:T(8,128)(2,1)S(1)}, bf16[768,2048]{1,0:T(8,128)(2,1)}, u32[]{:S(2)}) copy-start(bf16[768,2048]{1,0:T(8,128)(2,1)} %all-gather.2.cloned.1.call-done) | copy-start | bytes 9437188
  150.1 1.6 copy-start.4
  150.1 2.6 %copy-start.2 = (bf16[768,2048]{1,0:T(8,128)(2,1)}, bf16[768,2048]{1,0:T(8,128)(2,1)S(1)}, u32[]{:S(2)}) copy-start(bf16[768,2048]{1,0:T(8,128)(2,1)S(1)} %get-tuple-element.14) | copy-start | bytes 9437188
  158.4 19.1 %collective-permute-start.11 = (bf16[1024,256]{1,0:T(8,128)(2,1)}, bf16[1024,256]{1,0:T(8,128)(2,1)S(1)}, u32[]{:S(2)}, u32[]{:S(2)}) collective-permute-start(bf16[1024,256]{1,0:T(8,128)(2,1)} %bitcast.12), channel_id=1, source_target_pairs={{0,32},{32,64},{64,96},{96,0},{1,33},{33,65},{65,97},{97,1},{2,34}... | collective-permute-start | bytes 1572872 | tf_op jit(solution)/shard_map/ppermute | solution.py:23
  160.1 20.6 %collective-permute-start.12 = (bf16[1024,256]{1,0:T(8,128)(2,1)}, bf16[1024,256]{1,0:T(8,128)(2,1)S(1)}, u32[]{:S(2)}, u32[]{:S(2)}) collective-permute-start(bf16[1024,256]{1,0:T(8,128)(2,1)} %bitcast.12), channel_id=1, source_target_pairs={{0,96},{32,0},{64,32},{96,64},{1,97},{33,1},{65,33},{97,65},{2,98}... | collective-permute-start | bytes 1572872 | tf_op jit(solution)/shard_map/ppermute | solution.py:23
  160.4 20.4 %collective-permute-start.13 = (bf16[1024,256]{1,0:T(8,128)(2,1)}, bf16[1024,256]{1,0:T(8,128)(2,1)S(1)}, u32[]{:S(2)}, u32[]{:S(2)}) collective-permute-start(bf16[1024,256]{1,0:T(8,128)(2,1)} %bitcast.12), channel_id=1, source_target_pairs={{0,64},{32,96},{64,0},{96,32},{1,65},{33,97},{65,1},{97,33},{2,66}... | collective-permute-start | bytes 1572872 | tf_op jit(solution)/shard_map/ppermute | solution.py:23
  161.6 29.3 %all-to-all-start.4 = ((bf16[16,48,256]{2,1,0:T(8,128)(2,1)}), bf16[16,48,256]{2,1,0:T(8,128)(2,1)S(1)}, u32[]{:S(2)}, u32[]{:S(2)}) async-start(bf16[16,48,256]{2,1,0:T(8,128)(2,1)} %bitcast.19), calls=%async_computation.4 | async-start | bytes 786432 | tf_op jit(solution)/shard_map/all_to_all | solution.py:205
  168.3 12.5 %copy-start.5 = (bf16[768,2048]{1,0:T(8,128)(2,1)S(1)}, bf16[768,2048]{1,0:T(8,128)(2,1)}, u32[]{:S(2)}) copy-start(bf16[768,2048]{1,0:T(8,128)(2,1)} %copy-done.4) | copy-start | bytes 9437188
  180.8 1.9 copy-start.3
  182.7 14.9 %copy-start = (bf16[48,8192]{1,0:T(8,128)(2,1)S(1)}, bf16[48,8192]{1,0:T(8,128)(2,1)}, u32[]{:S(2)}) copy-start(bf16[48,8192]{1,0:T(8,128)(2,1)} %gate_ref.3) | copy-start | bytes 2359300
  190.8 29.9 %all-to-all-start.3 = ((bf16[16,48,256]{2,1,0:T(8,128)(2,1)}), bf16[16,48,256]{2,1,0:T(8,128)(2,1)S(1)}, u32[]{:S(2)}, u32[]{:S(2)}) async-start(bf16[16,48,256]{2,1,0:T(8,128)(2,1)} %bitcast.25), calls=%async_computation.3 | async-start | bytes 786432 | tf_op jit(solution)/shard_map/all_to_all | solution.py:205
Sparse Core Ops, SparseCore 0:
  9.8 109.5 all-gather.1
